TPU v7x, 256 devices: a whole 4x4x8 slice. The times are simulated.
256 devices in a mesh: rows: 128 (over y, z, x), cols: 2 (over core).
Axes of the slice: x: 4, y: 4, z: 8, core: 2. Of those that a mesh axis runs over, the one named last changes fastest.
Arguments:
- rhs: float32 [2, 768, 49152], P('cols', 'rows'), may hold values from -6 to 6
- pattern: int32 [384, 2], P(None, 'cols'), may hold values 0 or 1
- front_blocks: int32 [128, 4], replicated, may hold values from 0 to 383, as said below
- front_slot: int32 [128], replicated, may hold values from 0 to 255, as said below
- pivot_inverse: float32 [256, 256, 256], P('rows'), may hold values from -0.375 to 0.375
- update_factor: float32 [256, 256, 256], P('rows'), may hold values from -0.375 to 0.375
Outputs:
- solution: float32 [2, 768, 49152], P('cols', 'rows')
Inputs may be any that keep to these rules, and one draw needn't show every extreme that they name: `front_blocks`: columns 0 and 1 together name every row block that is no contribution block exactly once; columns 2 and 3 of a front are two different blocks, never a pivot block of any front. `front_slot`: all different; slot s belongs to index s // 2 of rows; some index holds 2 fronts in every draw; slots that no front names are unused.
All inputs are finite; a program needn't handle non-finite values. No bound on the sum of `pattern` on one device may be relied on, other than what follows from the above.
Results may differ from a plain program's by a relative error of at most 0.0001.
Values sent between devices are 32-bit elements; how exact they have to be, the bound alone decides.
A program may use at most 64 MiB of HBM per device.

v0:
```python
import jax
import jax.numpy as jnp
from jax import lax
from jax.sharding import PartitionSpec as P

BLOCK = 128
PIV = 256


def solve_slots(arrived, inverse_part, factor_part):
    width = inverse_part.shape[1]
    strict_lower = jnp.tril(jnp.ones((width, width), jnp.float32), -1)
    inverse = jnp.eye(width, dtype=jnp.float32)[None] + strict_lower[None] * inverse_part
    solved = jnp.einsum("kcj,kij->kci", arrived, inverse, precision=lax.Precision.HIGHEST)
    update = jnp.einsum("kcj,kij->kci", solved, factor_part, precision=lax.Precision.HIGHEST)
    return jnp.concatenate([solved, update], axis=2)


def on_device(rhs, pattern, front_blocks, front_slot, pivot_inverse, update_factor):
    fronts = front_blocks.shape[0]
    columns = rhs.shape[1]
    total_rows = rhs.shape[2]
    block_count = total_rows // BLOCK
    slot_dev = pivot_inverse.shape[0]
    devices = lax.axis_size("rows")
    pivot_blocks = front_blocks[:, :2].reshape(-1)
    contrib_blocks = front_blocks[:, 2:].reshape(-1)
    block_mask = pattern[:, 0].astype(jnp.float32)
    masked = rhs[0].reshape(columns, block_count, BLOCK) * block_mask[None, :, None]
    picked = jnp.swapaxes(
        jnp.take(masked, pivot_blocks, axis=1).reshape(columns, fronts, PIV), 0, 1
    )
    outbound = jnp.zeros((slot_dev * devices, columns, PIV), jnp.float32).at[front_slot].set(picked)
    arrived = lax.all_to_all(outbound, "rows", split_axis=0, concat_axis=1, tiled=True)
    worked = solve_slots(arrived, pivot_inverse, update_factor)
    returned = lax.all_to_all(worked, "rows", split_axis=1, concat_axis=0, tiled=True)
    gotten = returned[front_slot]
    solved = jnp.swapaxes(gotten[:, :, :PIV], 0, 1).reshape(columns, 2 * fronts, BLOCK)
    update = jnp.swapaxes(gotten[:, :, PIV:], 0, 1).reshape(columns, 2 * fronts, BLOCK)
    result = masked.at[:, pivot_blocks].set(solved)
    result = result.at[:, contrib_blocks].add(-update)
    return result.reshape(columns, total_rows)[None]


def solution(mesh):
    return jax.shard_map(
        on_device,
        mesh=mesh,
        in_specs=(
            P("cols", "rows", None),
            P(None, "cols"),
            P(),
            P(),
            P("rows", None, None),
            P("rows", None, None),
        ),
        out_specs=P("cols", "rows", None),
        check_vma=False,
    )
```

profile of v0, /device:TPU:1, one launch (start us, length us, event | category | flops | bytes accessed | tf_op | source)
XLA Modules:
  0.0 222.8 jit_solution(8477366295707670588)
XLA Ops:
  0.0 0.0 copy-start
  0.0 0.8 fusion.8
  0.8 0.7 compare_and_fusion
  1.5 0.1 copy.34
  1.6 0.1 reshape.108
  1.7 0.7 convert_reduce_fusion
  2.4 0.1 copy.35
  2.6 0.7 compare_select_fusion.3
  3.2 2.0 copy_multiply_fusion
  5.3 2.0 gather_fusion
  7.2 1.4 select_bitcast_fusion
  8.6 1.4 broadcast_in_dim.33
  10.1 13.7 %scatter_fusion = f32[256,6,256]{2,1,0:T(8,128)} fusion(f32[256,6,256]{2,1,0:T(8,128)} %broadcast_in_dim.33, s32[128]{0:T(128)S(1)} %compare_select_fusion.3, f32[128,6,256]{2,1,0:T(8,128)S(1)} %select_bitcast_fusion), kind=kCustom, calls=%fused_computation.2 | custom fusion | bytes 2359808 | tf_op jit(solution)/shard_map/scatter | solution.py:33
  23.8 16.9 %all-to-all-start = ((f32[256,6,256]{2,1,0:T(8,128)}), f32[256,6,256]{2,1,0:T(8,128)}, u32[]{:S(2)}, u32[]{:S(2)}) async-start(f32[256,6,256]{2,1,0:T(8,128)} %scatter_fusion), calls=%async_computation | async-start | bytes 4194304 | tf_op jit(solution)/shard_map/all_to_all | solution.py:34
  40.7 0.1 fusion.7
  40.8 48.8 %all-to-all-done = f32[256,6,256]{2,1,0:T(8,128)} async-done(((f32[256,6,256]{2,1,0:T(8,128)}), f32[256,6,256]{2,1,0:T(8,128)}, u32[]{:S(2)}, u32[]{:S(2)}) %all-to-all-start) | async-done | bytes 1572896 | tf_op jit(solution)/shard_map/all_to_all | solution.py:34
  89.6 2.5 %copy.36 = f32[128,2,6,256]{3,1,2,0:T(2,128)S(1)} copy(f32[128,2,6,256]{3,2,1,0:T(8,128)} %bitcast.6) | data formatting | bytes 3145728 | tf_op jit(solution)/shard_map/all_to_all | solution.py:34
  92.0 0.0 copy-done.1
  92.0 1.6 fusion
  93.7 1.6 fusion.9
  95.3 1.9 pad_maximum_fusion
  97.2 5.8 %copy.39 = f32[2,768,512]{2,0,1:T(2,128)} copy(f32[2,768,512]{1,2,0:T(8,128)} %pad_maximum_fusion) | data formatting | bytes 6291456 | tf_op jit(solution)/shard_map/concatenate | solution.py:16
  103.0 10.4 %all-to-all-start.1 = ((f32[2,768,512]{2,0,1:T(2,128)}), f32[2,768,512]{2,0,1:T(2,128)}, u32[]{:S(2)}, u32[]{:S(2)}) async-start(f32[2,768,512]{2,0,1:T(2,128)} %copy.39), calls=%async_computation.1 | async-start | bytes 6291456 | tf_op jit(solution)/shard_map/all_to_all | solution.py:36
  113.3 0.1 copy.42
  113.5 0.1 reshape.110
  113.6 70.3 %all-to-all-done.1 = f32[2,768,512]{2,0,1:T(2,128)} async-done(((f32[2,768,512]{2,0,1:T(2,128)}), f32[2,768,512]{2,0,1:T(2,128)}, u32[]{:S(2)}, u32[]{:S(2)}) %all-to-all-start.1) | async-done | bytes 3145760 | tf_op jit(solution)/shard_map/all_to_all | solution.py:36
  184.0 4.7 %copy.45 = f32[128,2,6,512]{3,2,1,0:T(8,128)} copy(f32[128,2,6,512]{3,1,2,0:T(2,128)} %bitcast.10) | data formatting | bytes 6291456 | tf_op jit(solution)/shard_map/all_to_all | solution.py:36
  188.7 4.2 %gather_fusion.1 = f32[128,6,512]{2,1,0:T(8,128)} fusion(f32[256,6,512]{2,1,0:T(8,128)} %bitcast.31, s32[1024]{0:T(1024)S(1)} %pad_clamp_fusion), kind=kCustom, calls=%fused_computation.1 | custom fusion | bytes 3146240 | tf_op jit(solution)/shard_map/gather | solution.py:37
  192.9 2.7 %slice_negate_fusion = (f32[128,6,256]{2,1,0:T(8,128)S(1)}, f32[128,6,256]{2,1,0:T(8,128)}) fusion(f32[128,6,512]{2,1,0:T(8,128)} %gather_fusion.1), kind=kLoop, calls=%fused_computation.9 | loop fusion | flops 196608 | bytes 3145728 | tf_op jit(solution)/shard_map/neg | solution.py:41
  195.6 16.7 %scatter_fusion.1 = f32[6,384,128]{2,0,1:T(8,128)S(1)} fusion(f32[6,384,128]{2,0,1:T(8,128)S(1)} %copy_multiply_fusion, s32[256]{0:T(256)S(1)} %bitcast.39, f32[256,6,128]{2,1,0:T(8,128)} %bitcast.35), kind=kCustom, calls=%fused_computation.3 | custom fusion | bytes 2360320 | tf_op jit(solution)/shard_map/scatter | solution.py:40
  212.3 8.3 %scatter_fusion.2 = f32[6,384,128]{2,0,1:T(8,128)S(1)} fusion(f32[6,384,128]{2,0,1:T(8,128)S(1)} %scatter_fusion.1, s32[256]{0:T(256)S(1)} %bitcast.40, f32[256,6,128]{2,1,0:T(8,128)S(1)} %bitcast.34), kind=kCustom, calls=%fused_computation.4 | custom fusion | flops 196608 | bytes 2360320 | tf_op jit(solution)/shard_map/scatter-add | solution.py:41
  220.6 2.2 copy.43
  (9 shorter events, 0.1 us)
Async XLA Ops:
  0.0 93.7 %copy-start = (f32[2,256,256]{2,1,0:T(8,128)S(1)}, f32[2,256,256]{2,1,0:T(8,128)}, u32[]{:S(2)}) copy-start(f32[2,256,256]{2,1,0:T(8,128)} %param.11) | copy-start | bytes 1572868
  23.8 65.8 %all-to-all-start = ((f32[256,6,256]{2,1,0:T(8,128)}), f32[256,6,256]{2,1,0:T(8,128)}, u32[]{:S(2)}, u32[]{:S(2)}) async-start(f32[256,6,256]{2,1,0:T(8,128)} %scatter_fusion), calls=%async_computation | async-start | bytes 4194304 | tf_op jit(solution)/shard_map/all_to_all | solution.py:34
  89.5 2.5 %copy-start.1 = (f32[2,256,256]{2,1,0:T(8,128)S(1)}, f32[2,256,256]{2,1,0:T(8,128)}, u32[]{:S(2)}) copy-start(f32[2,256,256]{2,1,0:T(8,128)} %param.10) | copy-start | bytes 1572868
  103.0 81.0 %all-to-all-start.1 = ((f32[2,768,512]{2,0,1:T(2,128)}), f32[2,768,512]{2,0,1:T(2,128)}, u32[]{:S(2)}, u32[]{:S(2)}) async-start(f32[2,768,512]{2,0,1:T(2,128)} %copy.39), calls=%async_computation.1 | async-start | bytes 6291456 | tf_op jit(solution)/shard_map/all_to_all | solution.py:36
where the time goes:
time: 227 us; the launch traced here: 223 us
  waiting for transfers between devices  119 us (52%)
  local copies, waits for them, and re-layouts  54.6 us (24%)
  starting transfers between devices  27.2 us (12%)
  other arithmetic  18.5 us (8%)
  matrix products  3.23 us (1%)
    all_to_all x1, waiting for transfers between devices, on_device(): lax.all_to_all(worked, 'rows', split_axis=1, concat_axis=0, tiled=True)  70.3 us
    all_to_all x1, waiting for transfers between devices, on_device(): lax.all_to_all(outbound, 'rows', split_axis=0, concat_axis=1, tiled=True)  48.8 us
    all_to_all x1, starting transfers between devices, on_device(): lax.all_to_all(outbound, 'rows', split_axis=0, concat_axis=1, tiled=True)  16.9 us
    scatter x1, local copies, waits for them, and re-layouts, on_device(): result = masked.at[:, pivot_blocks].set(solved)  16.7 us
    scatter x1, local copies, waits for them, and re-layouts, on_device(): jnp.zeros((slot_dev * devices, columns, PIV), jnp.float32).at[front_slot]  13.7 us
    all_to_all x1, starting transfers between devices, on_device(): lax.all_to_all(worked, 'rows', split_axis=1, concat_axis=0, tiled=True)  10.4 us
    scatter-add x1, other arithmetic, on_device(): result = result.at[:, contrib_blocks].add(-update)  8.31 us
    concatenate x1, local copies, waits for them, and re-layouts, solve_slots(): return jnp.concatenate([solved, update], axis=2)  5.78 us
  transfers between devices with their start and end apart: 2, of which 2 were waited for; matrix products, arithmetic and copies ran while one was open for 0% of the time, Pallas kernels for 0%

commit v1 on v0

v1 whole, which is shorter than its diff:
```python
import functools

import jax
import jax.numpy as jnp
from jax import lax
from jax.experimental import pallas as pl
from jax.experimental.pallas import tpu as pltpu
from jax.sharding import PartitionSpec as P

BLOCK = 128
PIV = 256
NX, NY, NZ = 4, 4, 8
PLANE = NX * NY
SLOT_DEV = 2
PAIRS = NZ
RING_SLOTS = NZ * SLOT_DEV
COLS = 6
MSG = COLS * 4
PACKED = 768
MESH = pl.DeviceIdType.MESH
PEERS = (
    (0, 1), (1, 0), (0, 3), (3, 0), (1, 1), (3, 3), (1, 3), (3, 1),
    (0, 2), (2, 0), (1, 2), (2, 1), (3, 2), (2, 3), (2, 2),
)


def nt(a, b):
    return lax.dot_general(a, b, (((1,), (1,)), ((), ())), preferred_element_type=jnp.float32)


def nn(a, b):
    return lax.dot_general(a, b, (((1,), (0,)), ((), ())), preferred_element_type=jnp.float32)


def split(v):
    high = v.astype(jnp.bfloat16)
    low = (v - high.astype(jnp.float32)).astype(jnp.bfloat16)
    return high, low


def product(dot, x, w):
    xh, xl = split(x)
    wh, wl = split(w)
    both = dot(jnp.concatenate([xh, xl], axis=0), wh)
    n = x.shape[0]
    return both[:n] + (both[n:] + dot(xh, wl))


def slot_place(slot, z):
    dev = lax.div(slot, SLOT_DEV)
    sl = lax.rem(slot, SLOT_DEV)
    ring = lax.div(dev, NX * NZ) * NX + lax.rem(dev, NX)
    zq = lax.rem(lax.div(dev, NX), NZ)
    delta = lax.rem(z - zq + NZ, NZ)
    near = jnp.minimum(delta, NZ - delta)
    above = (delta > NZ // 2).astype(jnp.int32)
    edge = jnp.logical_or(delta == 0, delta == NZ // 2)
    pair = jnp.where(delta == 0, 0, jnp.where(delta == NZ // 2, PAIRS - 1, 2 * near - 1 + lax.rem(sl + above, 2)))
    return ring, pair, jnp.where(edge, sl, above)


def prepare_kernel(slots, blocks, pattern, rhs, send):
    z = lax.rem(lax.div(lax.axis_index("rows"), NX), NZ)
    send[...] = jnp.zeros_like(send)

    def one_front(f, carry):
        ring, pair, a = slot_place(slots[f], z)
        for h in range(2):
            b = blocks[h, f]
            on = pattern[b].astype(jnp.float32)
            send[pair, ring, pl.ds(2 * a + h, COLS, stride=4), :] = rhs[:, b, :] * on
        return carry

    lax.fori_loop(0, slots.shape[0], one_front, 0, unroll=4)


def prepare(slots, blocks, pattern, rhs):
    vmem = pl.BlockSpec(memory_space=pltpu.VMEM)
    smem = pl.BlockSpec(memory_space=pltpu.SMEM)
    return pl.pallas_call(
        prepare_kernel,
        out_shape=jax.ShapeDtypeStruct((PAIRS, PLANE, MSG, BLOCK), jnp.float32),
        in_specs=[smem, smem, smem, vmem],
        out_specs=vmem,
        compiler_params=pltpu.CompilerParams(vmem_limit_bytes=16 * 1024 * 1024),
        name="prepare",
    )(slots, blocks, pattern, rhs)


def exchange_kernel(
    send, pinv, ufac, ret,
    fac, arr, back,
    ring_ss, ring_rs, core_ss, core_rs, out_ss, out_rs, ret_ss, ret_rs,
):
    r = lax.axis_index("rows")
    c = lax.axis_index("cols")
    x = lax.rem(r, NX)
    z = lax.rem(lax.div(r, NX), NZ)
    y = lax.div(r, NX * NZ)
    me = y * NX + x
    step_dir = 1 - 2 * c

    def chip(yy, zz, xx):
        return (yy * NZ + zz) * NX + xx

    def peer(dy, dx):
        return lax.rem(y + dy, NY), lax.rem(x + dx, NX)

    z_next = lax.rem(z + step_dir + NZ, NZ)
    z_prev = lax.rem(z - step_dir + NZ, NZ)

    barrier = pltpu.get_barrier_semaphore()
    for dy, dx in PEERS:
        py, px = peer(dy, dx)
        pl.semaphore_signal(barrier, inc=1, device_id=(chip(py, z, px), c), device_id_type=MESH)
    for zz in (z_next, z_prev):
        pl.semaphore_signal(barrier, inc=1, device_id=(chip(y, zz, x), c), device_id_type=MESH)
    pl.semaphore_signal(barrier, inc=1, device_id=(r, 1 - c), device_id_type=MESH)

    row = lax.broadcasted_iota(jnp.int32, (BLOCK, BLOCK), 0)
    col = lax.broadcasted_iota(jnp.int32, (BLOCK, BLOCK), 1)
    for s in range(SLOT_DEV):
        q = SLOT_DEV * z + s
        fac[q, 0:BLOCK, :] = jnp.where(
            row > col, pinv[s, :BLOCK, :BLOCK], pinv[s, BLOCK:, BLOCK:].T
        )
        fac[q, BLOCK : 2 * BLOCK, :] = pinv[s, BLOCK:, :BLOCK]
        fac[q, PIV : 2 * PIV, :] = ufac[s, :, :BLOCK]
        fac[q, 2 * PIV : 3 * PIV, :] = ufac[s, :, BLOCK:]

    pl.semaphore_wait(barrier, len(PEERS) + 3)

    def ring_copy(i):
        zs = lax.rem(z - step_dir * lax.div(i, 2) + NZ, NZ)
        q = SLOT_DEV * zs + lax.rem(i + c, 2)
        return pltpu.make_async_remote_copy(
            fac.at[q], fac.at[q], ring_ss.at[i], ring_rs.at[i],
            device_id=(chip(y, z_next, x), c), device_id_type=MESH,
        )

    def slot_from(i, cc):
        zs = lax.rem(z - (1 - 2 * cc) * (lax.div(i, 2) + 1) + NZ, NZ)
        return SLOT_DEV * zs + lax.rem(i + cc, 2)

    def core_copy(i, cc):
        q = slot_from(i, cc)
        return pltpu.make_async_remote_copy(
            fac.at[q], fac.at[q], core_ss.at[i], core_rs.at[i],
            device_id=(r, 1 - c), device_id_type=MESH,
        )

    def rows_at(ref, p, m):
        return ref.at[p, pl.ds(pl.multiple_of(m * MSG, 8), MSG), :]

    def start_out(p):
        for dy, dx in PEERS:
            py, px = peer(dy, dx)
            pltpu.make_async_remote_copy(
                send.at[p, py * NX + px], rows_at(arr, p, me), out_ss.at[p], out_rs.at[p],
                device_id=(chip(py, z, px), c), device_id_type=MESH,
            ).start()
        arr[p, pl.ds(pl.multiple_of(me * MSG, 8), MSG), :] = send[p, me]

    def start_back(t):
        for dy, dx in PEERS:
            py, px = peer(dy, dx)
            pltpu.make_async_remote_copy(
                rows_at(back, t, py * NX + px), rows_at(ret, t, me), ret_ss.at[t], ret_rs.at[t],
                device_id=(chip(py, z, px), c), device_id_type=MESH,
            ).start()
        pltpu.make_async_copy(rows_at(back, t, me), rows_at(ret, t, me), ret_rs.at[t]).start()

    def wait_bytes(ref, p, n, sem):
        view = ref.at[p, pl.ds(0, n * MSG), :]
        pltpu.make_async_copy(view, view, sem).wait()

    def solve(p, a, q):
        x0 = arr[p, pl.ds(2 * a, PLANE * COLS, stride=4), :]
        x1 = arr[p, pl.ds(2 * a + 1, PLANE * COLS, stride=4), :]
        merged = fac[q, 0:BLOCK, :]
        lower = jnp.where(row > col, merged, 0.0)
        upper = jnp.where(row < col, merged, 0.0)
        left = jnp.concatenate([lower, fac[q, BLOCK:PIV, :]], axis=0)
        first = product(nt, x0, left)
        y0 = x0 + first[:, :BLOCK]
        y1 = x1 + (first[:, BLOCK:] + product(nn, x1, upper))
        upd = product(nt, y0, fac[q, PIV : 2 * PIV, :]) + product(nt, y1, fac[q, 2 * PIV : 3 * PIV, :])
        t = 2 * p + a
        for h, v in enumerate((y0, y1, upd[:, :BLOCK], upd[:, BLOCK:])):
            back[t, pl.ds(h, PLANE * COLS, stride=4), :] = v
        start_back(t)

    ring_copy(0).start()
    ring_copy(1).start()
    start_out(0)

    def out_step(p, carry):
        start_out(p)
        return carry

    lax.fori_loop(1, PAIRS, out_step, 0)

    wait_bytes(arr, 0, PLANE - 1, out_rs.at[0])
    for a in range(2):
        solve(0, a, SLOT_DEV * z + a)

    def step(i, carry):
        ring_copy(i).wait_recv()

        @pl.when(i < PAIRS - 3)
        def _():
            ring_copy(i + 2).start()

        core_copy(i, c).start()
        wait_bytes(arr, i + 1, PLANE - 1, out_rs.at[i + 1])
        core_copy(i, 1 - c).wait_recv()
        solve(i + 1, 0, slot_from(i, 0))
        solve(i + 1, 1, slot_from(i, 1))
        return carry

    lax.fori_loop(0, PAIRS - 1, step, 0)

    def drain(i, carry):
        ring_copy(i).wait_send()
        core_copy(i, c).wait_send()
        return carry

    lax.fori_loop(0, PAIRS - 1, drain, 0)

    def drain_out(p, carry):
        wait_bytes(arr, p, PLANE - 1, out_ss.at[p])
        return carry

    lax.fori_loop(0, PAIRS, drain_out, 0)

    def drain_back(t, carry):
        wait_bytes(back, t, PLANE - 1, ret_ss.at[t])
        wait_bytes(back, t, PLANE, ret_rs.at[t])
        return carry

    lax.fori_loop(0, RING_SLOTS, drain_back, 0)


def exchange(send, pinv, ufac):
    vmem = pl.BlockSpec(memory_space=pltpu.VMEM)
    dma = pltpu.SemaphoreType.DMA
    return pl.pallas_call(
        exchange_kernel,
        out_shape=jax.ShapeDtypeStruct((RING_SLOTS, PLANE * MSG, BLOCK), jnp.float32),
        in_specs=[vmem, vmem, vmem],
        out_specs=pl.BlockSpec(memory_space=pl.ANY),
        scratch_shapes=[
            pltpu.VMEM((RING_SLOTS, PACKED, BLOCK), jnp.float32),
            pltpu.VMEM((PAIRS, PLANE * MSG, BLOCK), jnp.float32),
            pltpu.VMEM((RING_SLOTS, PLANE * MSG, BLOCK), jnp.float32),
            dma((PAIRS - 1,)), dma((PAIRS - 1,)), dma((PAIRS - 1,)), dma((PAIRS - 1,)),
            dma((PAIRS,)), dma((PAIRS,)), dma((RING_SLOTS,)), dma((RING_SLOTS,)),
        ],
        compiler_params=pltpu.CompilerParams(
            collective_id=0, has_side_effects=True, vmem_limit_bytes=40 * 1024 * 1024
        ),
        name="exchange",
    )(send, pinv, ufac)


def assemble_kernel(slots, blocks, pattern, rhs, ret, out):
    z = lax.rem(lax.div(lax.axis_index("rows"), NX), NZ)

    def mask_one(b, carry):
        on = pattern[b].astype(jnp.float32)
        out[:, b, :] = rhs[:, b, :] * on
        return carry

    lax.fori_loop(0, pattern.shape[0], mask_one, 0, unroll=8)

    def one_front(f, carry):
        ring, pair, a = slot_place(slots[f], z)
        at = (2 * pair + a) * PLANE + ring
        for h in range(4):
            b = blocks[h, f]
            v = ret[at, pl.ds(h, COLS, stride=4), :]
            if h < 2:
                out[:, b, :] = v
            else:
                out[:, b, :] = out[:, b, :] - v
        return carry

    lax.fori_loop(0, slots.shape[0], one_front, 0, unroll=2)


def assemble(slots, blocks, pattern, rhs, ret):
    vmem = pl.BlockSpec(memory_space=pltpu.VMEM)
    smem = pl.BlockSpec(memory_space=pltpu.SMEM)
    return pl.pallas_call(
        assemble_kernel,
        out_shape=jax.ShapeDtypeStruct(rhs.shape, jnp.float32),
        in_specs=[smem, smem, smem, vmem, vmem],
        out_specs=vmem,
        compiler_params=pltpu.CompilerParams(vmem_limit_bytes=16 * 1024 * 1024),
        name="assemble",
    )(slots, blocks, pattern, rhs, ret)


def on_device(rhs, pattern, front_blocks, front_slot, pivot_inverse, update_factor):
    shape = rhs.shape
    pattern = pattern.reshape(-1)
    blocks = front_blocks.T
    rhs = rhs.reshape(COLS, -1, BLOCK)
    send = prepare(front_slot, blocks, pattern, rhs)
    ret = exchange(send, pivot_inverse, update_factor)
    ret = ret.reshape(RING_SLOTS * PLANE, MSG, BLOCK)
    return assemble(front_slot, blocks, pattern, rhs, ret).reshape(shape)


def solution(mesh):
    return jax.shard_map(
        on_device,
        mesh=mesh,
        in_specs=(
            P("cols", "rows", None),
            P(None, "cols"),
            P(),
            P(),
            P("rows", None, None),
            P("rows", None, None),
        ),
        out_specs=P("cols", "rows", None),
        check_vma=False,
    )
```

time: 227 us -> 78.4 us (0.35); the launches traced: 223 us -> 78.3 us
  waiting for transfers between devices: 119 us -> 0 us
  Pallas kernels: 0 us -> 74.8 us
  local copies, waits for them, and re-layouts: 54.6 us -> 2.63 us
  starting transfers between devices: 27.2 us -> 0 us
  other arithmetic: 18.5 us -> 0.7 us
  matrix products: 3.23 us -> 0 us
    all_to_all x2 -> x0, waiting for transfers between devices: 119 us -> none  [the longest x1 70.3 us: on_device(): lax.all_to_all(worked, 'rows', split_axis=1, concat_axis=0, tiled=True)]
    pallas_call x0 -> x3, Pallas kernels: none -> 74.8 us  [the longest x1 63.4 us: exchange(): pl.pallas_call(exchange_kernel, out_shape=jax.ShapeDtypeStruct((RING_SLOT...]
    scatter x2 -> x0, local copies, waits for them, and re-layouts: 30.4 us -> none  [the longest x1 16.7 us: on_device(): result = masked.at[:, pivot_blocks].set(solved)]
    all_to_all x2 -> x0, starting transfers between devices: 27.2 us -> none  [the longest x1 16.9 us: on_device(): lax.all_to_all(outbound, 'rows', split_axis=0, concat_axis=1, tiled=True)]
    scatter-add x1 -> x0, other arithmetic: 8.31 us -> none  [on_device(): result = result.at[:, contrib_blocks].add(-update)]
    all_to_all x2 -> x0, local copies, waits for them, and re-layouts: 7.17 us -> none  [the longest x1 4.72 us: on_device(): lax.all_to_all(worked, 'rows', split_axis=1, concat_axis=0, tiled=True)]
    gather x2 -> x0, local copies, waits for them, and re-layouts: 6.19 us -> none  [the longest x1 4.2 us: on_device(): gotten = returned[front_slot]]
    concatenate x1 -> x0, local copies, waits for them, and re-layouts: 5.78 us -> none  [solve_slots(): return jnp.concatenate([solved, update], axis=2)]
  transfers between devices with their start and end apart: 2 -> 0, of which waited for: 2 -> 0; matrix products, arithmetic and copies ran while one was open for 0% -> 0% of each run, Pallas kernels for 0% -> 0%
where the time goes in v1:
time: 78.4 us; the launch traced here: 78.3 us
  Pallas kernels  74.8 us (95%)
  local copies, waits for them, and re-layouts  2.63 us (3%)
    pallas_call x1, Pallas kernels, exchange(): pl.pallas_call(exchange_kernel, out_shape=jax.ShapeDtypeStruct((RING_SLOT...  63.4 us
    pallas_call x1, Pallas kernels, assemble(): pl.pallas_call(assemble_kernel, out_shape=jax.ShapeDtypeStruct(rhs.shape,...  7.87 us
    pallas_call x1, Pallas kernels, prepare(): pl.pallas_call(prepare_kernel, out_shape=jax.ShapeDtypeStruct((PAIRS, PLA...  3.52 us
    unnamed x16, local copies, waits for them, and re-layouts  2.63 us

profile of v1, /device:TPU:1, one launch (start us, length us, event | category | flops | bytes accessed | tf_op | source)
XLA Modules:
  0.0 78.3 jit_solution(17896788979116123831)
XLA Ops:
  0.0 0.7 reduce.pattern
  0.7 0.0 copy-start
  0.7 1.3 %copy-done = f32[1,6,49152]{2,0,1:T(1,128)S(1)} copy-done((f32[1,6,49152]{2,0,1:T(1,128)S(1)}, f32[1,6,49152]{2,0,1:T(1,128)}, u32[]{:S(2)}) %copy-start) | copy-done | bytes 1179672
  2.0 0.0 copy-start.4
  2.0 0.7 copy-done.4
  2.7 0.0 copy-start.6
  2.7 0.7 copy-done.6
  3.3 0.0 copy-start.2
  3.3 0.0 copy-start.3
  3.3 3.5 %prepare.1.send = f32[8,16,24,128]{3,2,1,0:T(8,128)S(1)} custom-call(s32[128]{0:T(128)S(1)} %copy-done.6, s32[4,128]{1,0:T(4,128)S(1)} %bitcast.7, s32[384]{0:T(512)S(1)} %reduce.pattern, f32[6,384,128]{2,1,0:T(8,128)S(1)} %bitcast.5), custom_call_target="tpu_custom_call" | custom-call | tf_op jit(solution)/shard_map/prepare/pallas_call | solution.py:80
  6.8 0.0 copy-done.2
  6.9 0.0 copy-done.3
  6.9 0.0 copy-start.1
  6.9 0.0 copy-start.5
  6.9 0.0 copy-start.7
  6.9 63.4 %exchange.1 = f32[16,384,128]{2,1,0:T(8,128)S(1)} custom-call(f32[8,16,24,128]{3,2,1,0:T(8,128)S(1)} %prepare.1.send, f32[2,256,256]{2,1,0:T(8,128)S(1)} %copy-done.2, f32[2,256,256]{2,1,0:T(8,128)S(1)} %copy-done.3), custom_call_target="tpu_custom_call" | custom-call | tf_op jit(solution)/shard_map/exchange/pallas_call | solution.py:247
  70.4 0.0 copy-done.1
  70.4 0.0 copy-done.5
  70.4 0.0 copy-done.7
  70.4 7.9 %assemble.1 = f32[6,384,128]{2,1,0:T(8,128)} custom-call(s32[128]{0:T(128)S(1)} %copy-done.7, s32[4,128]{1,0:T(4,128)S(1)} %bitcast.8, s32[384]{0:T(512)S(1)} %reduce.pattern, f32[6,384,128]{2,1,0:T(8,128)S(1)} %bitcast.6, f32[256,24,128]{2,1,0:T(8,128)S(1)} %bitcast.4), custom_call_target="tpu_custom_call" | custom-call | tf_op jit(solution)/shard_map/assemble/pallas_call | solution.py:294
Async XLA Ops:
  0.7 1.3 %copy-start = (f32[1,6,49152]{2,0,1:T(1,128)S(1)}, f32[1,6,49152]{2,0,1:T(1,128)}, u32[]{:S(2)}) copy-start(f32[1,6,49152]{2,0,1:T(1,128)} %param.6) | copy-start | bytes 3538948
  2.0 0.7 copy-start.4
  2.7 0.7 copy-start.6
  3.3 3.5 %copy-start.2 = (f32[2,256,256]{2,1,0:T(8,128)S(1)}, f32[2,256,256]{2,1,0:T(8,128)}, u32[]{:S(2)}) copy-start(f32[2,256,256]{2,1,0:T(8,128)} %pinv.1) | copy-start | bytes 1572868
  3.3 3.5 %copy-start.3 = (f32[2,256,256]{2,1,0:T(8,128)S(1)}, f32[2,256,256]{2,1,0:T(8,128)}, u32[]{:S(2)}) copy-start(f32[2,256,256]{2,1,0:T(8,128)} %ufac.1) | copy-start | bytes 1572868
  6.9 63.5 %copy-start.1 = (f32[1,6,49152]{2,0,1:T(1,128)S(1)}, f32[1,6,49152]{2,0,1:T(1,128)}, u32[]{:S(2)}) copy-start(f32[1,6,49152]{2,0,1:T(1,128)} %param.6) | copy-start | bytes 3538948
  6.9 63.5 %copy-start.5 = (s32[128,4]{0,1:T(4,128)S(1)}, s32[128,4]{0,1:T(4,128)}, u32[]{:S(2)}) copy-start(s32[128,4]{0,1:T(4,128)} %param.8) | copy-start | bytes 6148
  6.9 63.5 %copy-start.7 = (s32[128]{0:T(128)S(1)}, s32[128]{0:T(128)}, u32[]{:S(2)}) copy-start(s32[128]{0:T(128)} %slots.3) | copy-start | bytes 1540

commit v2 on v1

--- a/solution.py
+++ b/solution.py
@@ -15,7 +15,9 @@
 PAIRS = NZ
 RING_SLOTS = NZ * SLOT_DEV
 COLS = 6
+ROW_BLOCKS = 384
 MSG = COLS * 4
+NEAR = 2
 PACKED = 768
 MESH = pl.DeviceIdType.MESH
 PEERS = (
@@ -46,50 +48,111 @@
     return both[:n] + (both[n:] + dot(xh, wl))
 
 
-def slot_place(slot, z):
-    dev = lax.div(slot, SLOT_DEV)
-    sl = lax.rem(slot, SLOT_DEV)
-    ring = lax.div(dev, NX * NZ) * NX + lax.rem(dev, NX)
-    zq = lax.rem(lax.div(dev, NX), NZ)
-    delta = lax.rem(z - zq + NZ, NZ)
-    near = jnp.minimum(delta, NZ - delta)
-    above = (delta > NZ // 2).astype(jnp.int32)
-    edge = jnp.logical_or(delta == 0, delta == NZ // 2)
-    pair = jnp.where(delta == 0, 0, jnp.where(delta == NZ // 2, PAIRS - 1, 2 * near - 1 + lax.rem(sl + above, 2)))
-    return ring, pair, jnp.where(edge, sl, above)
-
-
-def prepare_kernel(slots, blocks, pattern, rhs, send):
+TIERS = (12, 14, 16)
+
+
+def first_position(tier, p):
+    if tier == 12:
+        return max(p - 1, 0) if p < 3 else 2 * p - 4
+    return max(2 * p - (16 - tier), 0)
+
+
+def slot_in_sequence(o, z, ring):
+    p, a = o // 2, o % 2
+    i = p - 1
+    reach = (i >> 1) + 1
+    zs = jnp.where(p == 0, z, jnp.where(a == 0, z - reach, z + reach)) & (NZ - 1)
+    sl = jnp.where(p == 0, a, (i + a) & 1)
+    return (((ring >> 2) * NZ + zs) * NX + (ring & (NX - 1))) * SLOT_DEV + sl
+
+
+def prepare_kernel(slots, blocks, mask, rhs, send, table, tier_ref, table_s, sem):
     z = lax.rem(lax.div(lax.axis_index("rows"), NX), NZ)
+    shape = (RING_SLOTS, 128)
+    o_of = lax.broadcasted_iota(jnp.int32, shape, 0)
+    lane = lax.broadcasted_iota(jnp.int32, shape, 1)
+    slot_of = slot_in_sequence(o_of, lane >> 4, lane & 15)
+
+    def mark(f, occ):
+        for k in range(8):
+            occ = jnp.where(slot_of == slots[8 * f + k], 1, occ)
+        return occ
+
+    occ = lax.fori_loop(0, slots.shape[0] // 8, mark, jnp.zeros(shape, jnp.int32))
+    used = occ > 0
+    count = jnp.zeros((1, 128), jnp.int32)
+    ranks = []
+    last = {t: jnp.full((1, 128), -1, jnp.int32) for t in TIERS}
+    places = {t: [] for t in TIERS}
+    for o in range(RING_SLOTS):
+        on = used[o : o + 1]
+        ranks.append(jnp.where(on, count, 0))
+        count = count + occ[o : o + 1]
+        for t in TIERS:
+            last[t] = jnp.where(on, jnp.maximum(last[t] + 1, first_position(t, o // 2)), last[t])
+            places[t].append(jnp.where(on, last[t], 255))
+    rank = jnp.concatenate(ranks, axis=0)
+    fits = [jnp.max(last[t]) < t for t in TIERS]
+    tier = jnp.where(fits[0], 0, jnp.where(fits[1], 1, 2))
+    place = {t: jnp.concatenate(places[t], axis=0) for t in TIERS}
+    place = jnp.where(tier == 0, place[TIERS[0]], jnp.where(tier == 1, place[TIERS[1]], place[TIERS[2]]))
+    holds = jnp.zeros(shape, jnp.int32)
+    for o in range(RING_SLOTS):
+        holds = jnp.where(place[o : o + 1] == o_of, o, holds)
+    table[...] = rank + (place << 8) + (holds << 16)
+    tier_ref[0] = tier
+    copy = pltpu.make_async_copy(table, table_s, sem)
+    copy.start()
     send[...] = jnp.zeros_like(send)
+    copy.wait()
 
     def one_front(f, carry):
-        ring, pair, a = slot_place(slots[f], z)
+        o, ring = sequence_of(slots[f], z)
+        k = table_s[o, z * PLANE + ring] & 255
         for h in range(2):
             b = blocks[h, f]
-            on = pattern[b].astype(jnp.float32)
-            send[pair, ring, pl.ds(2 * a + h, COLS, stride=4), :] = rhs[:, b, :] * on
+            v = rhs[pl.ds(b, COLS, stride=ROW_BLOCKS), :] * mask[pl.ds(b, 1), :]
+            send[k >> 1, ring, pl.ds(2 * (k & 1) + h, COLS, stride=4), :] = v
         return carry
 
     lax.fori_loop(0, slots.shape[0], one_front, 0, unroll=4)
 
 
-def prepare(slots, blocks, pattern, rhs):
+def sequence_of(slot, z):
+    sl = slot & 1
+    ring = ((slot >> 6) << 2) + ((slot >> 1) & 3)
+    delta = (z - (slot >> 3)) & (NZ - 1)
+    near = jnp.minimum(delta, NZ - delta)
+    above = jnp.where(delta > NZ // 2, 1, 0)
+    o = 4 * near - 2 + 2 * (sl ^ above) + above
+    o = jnp.where(delta == NZ // 2, 2 * (PAIRS - 1) + sl, o)
+    return jnp.where(delta == 0, sl, o), ring
+
+
+def prepare(slots, blocks, mask, rhs):
     vmem = pl.BlockSpec(memory_space=pltpu.VMEM)
     smem = pl.BlockSpec(memory_space=pltpu.SMEM)
     return pl.pallas_call(
         prepare_kernel,
-        out_shape=jax.ShapeDtypeStruct((PAIRS, PLANE, MSG, BLOCK), jnp.float32),
-        in_specs=[smem, smem, smem, vmem],
-        out_specs=vmem,
+        out_shape=(
+            jax.ShapeDtypeStruct((PAIRS, PLANE, MSG, BLOCK), jnp.float32),
+            jax.ShapeDtypeStruct((RING_SLOTS, 128), jnp.int32),
+            jax.ShapeDtypeStruct((1,), jnp.int32),
+        ),
+        in_specs=[smem, smem, vmem, vmem],
+        out_specs=(vmem, vmem, smem),
+        scratch_shapes=[
+            pltpu.SMEM((RING_SLOTS, 128), jnp.int32),
+            pltpu.SemaphoreType.DMA,
+        ],
         compiler_params=pltpu.CompilerParams(vmem_limit_bytes=16 * 1024 * 1024),
         name="prepare",
-    )(slots, blocks, pattern, rhs)
+    )(slots, blocks, mask, rhs)
 
 
 def exchange_kernel(
-    send, pinv, ufac, ret,
-    fac, arr, back,
+    tier, table, send, pinv, ufac, ret,
+    fac, near, arr, res, back,
     ring_ss, ring_rs, core_ss, core_rs, out_ss, out_rs, ret_ss, ret_rs,
 ):
     r = lax.axis_index("rows")
@@ -152,14 +215,14 @@
     def rows_at(ref, p, m):
         return ref.at[p, pl.ds(pl.multiple_of(m * MSG, 8), MSG), :]
 
-    def start_out(p):
+    def start_out(p, into):
         for dy, dx in PEERS:
             py, px = peer(dy, dx)
             pltpu.make_async_remote_copy(
-                send.at[p, py * NX + px], rows_at(arr, p, me), out_ss.at[p], out_rs.at[p],
+                send.at[p, py * NX + px], rows_at(into, p, me), out_ss.at[p], out_rs.at[p],
                 device_id=(chip(py, z, px), c), device_id_type=MESH,
             ).start()
-        arr[p, pl.ds(pl.multiple_of(me * MSG, 8), MSG), :] = send[p, me]
+        into[p, pl.ds(pl.multiple_of(me * MSG, 8), MSG), :] = send[p, me]
 
     def start_back(t):
         for dy, dx in PEERS:
@@ -174,9 +237,20 @@
         view = ref.at[p, pl.ds(0, n * MSG), :]
         pltpu.make_async_copy(view, view, sem).wait()
 
-    def solve(p, a, q):
-        x0 = arr[p, pl.ds(2 * a, PLANE * COLS, stride=4), :]
-        x1 = arr[p, pl.ds(2 * a + 1, PLANE * COLS, stride=4), :]
+    lane = z * PLANE + me
+
+    def solve(o, q, data):
+        k = table[o, lane] & 255
+        data = data.at[k >> 1]
+        second = (k & 1) == 1
+        x0, x1 = (
+            jnp.where(
+                second,
+                data[pl.ds(2 + h, PLANE * COLS, stride=4), :],
+                data[pl.ds(h, PLANE * COLS, stride=4), :],
+            )
+            for h in range(2)
+        )
         merged = fac[q, 0:BLOCK, :]
         lower = jnp.where(row > col, merged, 0.0)
         upper = jnp.where(row < col, merged, 0.0)
@@ -185,26 +259,33 @@
         y0 = x0 + first[:, :BLOCK]
         y1 = x1 + (first[:, BLOCK:] + product(nn, x1, upper))
         upd = product(nt, y0, fac[q, PIV : 2 * PIV, :]) + product(nt, y1, fac[q, 2 * PIV : 3 * PIV, :])
-        t = 2 * p + a
         for h, v in enumerate((y0, y1, upd[:, :BLOCK], upd[:, BLOCK:])):
-            back[t, pl.ds(h, PLANE * COLS, stride=4), :] = v
+            res[o, pl.ds(h, PLANE * COLS, stride=4), :] = v
+
+    def give_back(t):
+        back[t] = res[table[t, lane] >> 16]
         start_back(t)
 
     ring_copy(0).start()
     ring_copy(1).start()
-    start_out(0)
+    for p in range(NEAR):
+        start_out(p, near)
 
     def out_step(p, carry):
-        start_out(p)
-        return carry
-
-    lax.fori_loop(1, PAIRS, out_step, 0)
-
-    wait_bytes(arr, 0, PLANE - 1, out_rs.at[0])
+        start_out(p, arr)
+        return carry
+
+    lax.fori_loop(NEAR, tier // 2, out_step, 0)
+
+    for p in range(NEAR):
+        wait_bytes(near, p, PLANE - 1, out_rs.at[p])
     for a in range(2):
-        solve(0, a, SLOT_DEV * z + a)
-
-    def step(i, carry):
+        solve(a, SLOT_DEV * z + a, near)
+    if first_position(tier, 1) > 0:
+        for t in range(first_position(tier, 1)):
+            give_back(t)
+
+    def advance(i):
         ring_copy(i).wait_recv()
 
         @pl.when(i < PAIRS - 3)
@@ -212,13 +293,41 @@
             ring_copy(i + 2).start()
 
         core_copy(i, c).start()
-        wait_bytes(arr, i + 1, PLANE - 1, out_rs.at[i + 1])
         core_copy(i, 1 - c).wait_recv()
-        solve(i + 1, 0, slot_from(i, 0))
-        solve(i + 1, 1, slot_from(i, 1))
-        return carry
-
-    lax.fori_loop(0, PAIRS - 1, step, 0)
+
+    advance(jnp.int32(0))
+    for a in range(2):
+        solve(2 + a, slot_from(jnp.int32(0), a), near)
+    for t in range(first_position(tier, 1), first_position(tier, 2)):
+        give_back(t)
+
+    for p in range(NEAR):
+        arr[p] = near[p]
+
+    def arrive(p, carry):
+        wait_bytes(arr, p, PLANE - 1, out_rs.at[p])
+        return carry
+
+    lax.fori_loop(NEAR, tier // 2, arrive, 0)
+
+    def step(i, carry):
+        advance(i)
+        for a in range(2):
+            solve(2 * i + 2 + a, slot_from(i, a), arr)
+        p = i + 1
+        if tier == 12:
+            t = jnp.where(p < 3, p - 1, 2 * p - 4)
+        else:
+            t = 2 * p - (16 - tier)
+        give_back(t)
+
+        @pl.when(p >= (3 if tier == 12 else 0))
+        def _():
+            give_back(t + 1)
+
+        return carry
+
+    lax.fori_loop(1, PAIRS - 1, step, 0)
 
     def drain(i, carry):
         ring_copy(i).wait_send()
@@ -231,85 +340,85 @@
         wait_bytes(arr, p, PLANE - 1, out_ss.at[p])
         return carry
 
-    lax.fori_loop(0, PAIRS, drain_out, 0)
+    lax.fori_loop(0, tier // 2, drain_out, 0)
 
     def drain_back(t, carry):
         wait_bytes(back, t, PLANE - 1, ret_ss.at[t])
         wait_bytes(back, t, PLANE, ret_rs.at[t])
         return carry
 
-    lax.fori_loop(0, RING_SLOTS, drain_back, 0)
-
-
-def exchange(send, pinv, ufac):
+    lax.fori_loop(0, tier, drain_back, 0)
+
+
+def exchange(tier, table, send, pinv, ufac):
     vmem = pl.BlockSpec(memory_space=pltpu.VMEM)
     dma = pltpu.SemaphoreType.DMA
     return pl.pallas_call(
-        exchange_kernel,
+        functools.partial(exchange_kernel, tier),
         out_shape=jax.ShapeDtypeStruct((RING_SLOTS, PLANE * MSG, BLOCK), jnp.float32),
-        in_specs=[vmem, vmem, vmem],
+        in_specs=[pl.BlockSpec(memory_space=pltpu.SMEM), vmem, vmem, vmem],
         out_specs=pl.BlockSpec(memory_space=pl.ANY),
         scratch_shapes=[
             pltpu.VMEM((RING_SLOTS, PACKED, BLOCK), jnp.float32),
+            pltpu.VMEM((NEAR, PLANE * MSG, BLOCK), jnp.float32),
             pltpu.VMEM((PAIRS, PLANE * MSG, BLOCK), jnp.float32),
+            pltpu.VMEM((RING_SLOTS, PLANE * MSG, BLOCK), jnp.float32),
             pltpu.VMEM((RING_SLOTS, PLANE * MSG, BLOCK), jnp.float32),
             dma((PAIRS - 1,)), dma((PAIRS - 1,)), dma((PAIRS - 1,)), dma((PAIRS - 1,)),
             dma((PAIRS,)), dma((PAIRS,)), dma((RING_SLOTS,)), dma((RING_SLOTS,)),
         ],
         compiler_params=pltpu.CompilerParams(
-            collective_id=0, has_side_effects=True, vmem_limit_bytes=40 * 1024 * 1024
+            collective_id=TIERS.index(tier), has_side_effects=True, vmem_limit_bytes=40 * 1024 * 1024
         ),
-        name="exchange",
-    )(send, pinv, ufac)
-
-
-def assemble_kernel(slots, blocks, pattern, rhs, ret, out):
+        name=f"exchange_{tier}",
+    )(table, send, pinv, ufac)
+
+
+def assemble_kernel(table, slots, blocks, mask, rhs, ret, out):
     z = lax.rem(lax.div(lax.axis_index("rows"), NX), NZ)
-
-    def mask_one(b, carry):
-        on = pattern[b].astype(jnp.float32)
-        out[:, b, :] = rhs[:, b, :] * on
-        return carry
-
-    lax.fori_loop(0, pattern.shape[0], mask_one, 0, unroll=8)
+    for j in range(COLS):
+        rows = pl.ds(j * ROW_BLOCKS, ROW_BLOCKS)
+        out[rows, :] = rhs[rows, :] * mask[...]
 
     def one_front(f, carry):
-        ring, pair, a = slot_place(slots[f], z)
-        at = (2 * pair + a) * PLANE + ring
+        o, ring = sequence_of(slots[f], z)
+        at = ((table[o, z * PLANE + ring] >> 8) & 255) * PLANE + ring
         for h in range(4):
-            b = blocks[h, f]
+            rows = pl.ds(blocks[h, f], COLS, stride=ROW_BLOCKS)
             v = ret[at, pl.ds(h, COLS, stride=4), :]
             if h < 2:
-                out[:, b, :] = v
+                out[rows, :] = v
             else:
-                out[:, b, :] = out[:, b, :] - v
+                out[rows, :] = out[rows, :] - v
         return carry
 
     lax.fori_loop(0, slots.shape[0], one_front, 0, unroll=2)
 
 
-def assemble(slots, blocks, pattern, rhs, ret):
+def assemble(table, slots, blocks, mask, rhs, ret):
     vmem = pl.BlockSpec(memory_space=pltpu.VMEM)
     smem = pl.BlockSpec(memory_space=pltpu.SMEM)
     return pl.pallas_call(
         assemble_kernel,
         out_shape=jax.ShapeDtypeStruct(rhs.shape, jnp.float32),
-        in_specs=[smem, smem, smem, vmem, vmem],
+        in_specs=[smem, smem, smem, vmem, vmem, vmem],
         out_specs=vmem,
         compiler_params=pltpu.CompilerParams(vmem_limit_bytes=16 * 1024 * 1024),
         name="assemble",
-    )(slots, blocks, pattern, rhs, ret)
+    )(table, slots, blocks, mask, rhs, ret)
 
 
 def on_device(rhs, pattern, front_blocks, front_slot, pivot_inverse, update_factor):
     shape = rhs.shape
-    pattern = pattern.reshape(-1)
+    mask = jnp.broadcast_to(pattern.astype(jnp.float32), (ROW_BLOCKS, BLOCK))
     blocks = front_blocks.T
-    rhs = rhs.reshape(COLS, -1, BLOCK)
-    send = prepare(front_slot, blocks, pattern, rhs)
-    ret = exchange(send, pivot_inverse, update_factor)
+    rhs = rhs.reshape(COLS * ROW_BLOCKS, BLOCK)
+    send, table, tier = prepare(front_slot, blocks, mask, rhs)
+    ret = lax.switch(
+        tier[0], [functools.partial(exchange, t) for t in TIERS], table, send, pivot_inverse, update_factor
+    )
     ret = ret.reshape(RING_SLOTS * PLANE, MSG, BLOCK)
-    return assemble(front_slot, blocks, pattern, rhs, ret).reshape(shape)
+    return assemble(table, front_slot, blocks, mask, rhs, ret).reshape(shape)
 
 
 def solution(mesh):

time: 78.4 us -> 76.9 us (0.981); the launches traced: 78.3 us -> 77.7 us
  Pallas kernels: 74.8 us -> 73.5 us
    pallas_call x1, Pallas kernels: 7.87 us -> 7.02 us  [assemble(): pl.pallas_call(assemble_kernel, out_shape=jax.ShapeDtypeStruct(rhs.shape,...]
    unnamed x16 -> x12, local copies, waits for them, and re-layouts: 2.63 us -> 2.62 us
where the time goes in v2:
time: 76.9 us; the launch traced here: 77.7 us
  Pallas kernels  73.5 us (96%)
  local copies, waits for them, and re-layouts  2.73 us (4%)
    pallas_call x1, Pallas kernels, exchange(): pl.pallas_call(functools.partial(exchange_kernel, tier), out_shape=jax.Sh...  62.1 us
    pallas_call x1, Pallas kernels, assemble(): pl.pallas_call(assemble_kernel, out_shape=jax.ShapeDtypeStruct(rhs.shape,...  7.02 us
    pallas_call x1, Pallas kernels, prepare(): pl.pallas_call(prepare_kernel, out_shape=(jax.ShapeDtypeStruct((PAIRS, PL...  4.43 us
    unnamed x12, local copies, waits for them, and re-layouts  2.62 us

profile of v2, /device:TPU:1, one launch (start us, length us, event | category | flops | bytes accessed | tf_op | source)
XLA Modules:
  0.0 77.7 jit_solution(10415367917164538051)
XLA Ops:
  0.0 0.7 convert_reduce_fusion
  0.7 0.1 broadcast_in_dim.8.mask
  0.8 0.0 copy-start
  0.8 1.3 %copy-done = f32[1,6,49152]{2,0,1:T(1,128)S(1)} copy-done((f32[1,6,49152]{2,0,1:T(1,128)S(1)}, f32[1,6,49152]{2,0,1:T(1,128)}, u32[]{:S(2)}) %copy-start) | copy-done | bytes 1179672
  2.1 0.0 copy-start.2
  2.1 0.7 copy-done.2
  2.8 0.0 copy-start.4
  2.8 0.7 copy-done.4
  3.4 4.4 %prepare.1 = (f32[8,16,24,128]{3,2,1,0:T(8,128)S(1)}, s32[16,128]{1,0:T(8,128)S(1)}, s32[1]{0:T(128)}) custom-call(s32[128]{0:T(128)S(1)} %copy-done.4, s32[4,128]{1,0:T(4,128)S(1)} %bitcast.9, f32[384,128]{1,0:T(8,128)S(1)} %broadcast_in_dim.8.mask, f32[2304,128]{1,0:T(8,128)S(1)} %bitcast.7), custom_call_target="tpu_custom_call" | custom-call | tf_op jit(solution)/shard_map/prepare/pallas_call | solution.py:135
  8.5 0.0 copy-start.1
  8.5 0.0 copy-start.3
  8.5 0.0 copy-start.5
  8.6 62.1 %conditional.1 = (f32[256,24,128]{2,1,0:T(8,128)}) conditional(s32[]{:T(128)} %bitcast.5, (s32[16,128]{1,0:T(8,128)S(1)}, f32[8,16,24,128]{3,2,1,0:T(8,128)S(1)}, f32[2,256,256]{2,1,0:T(8,128)}, f32[2,256,256]{2,1,0:T(8,128)}) %tuple.17, (s32[16,128]{1,0:T(8,128)S(1)}, f32[8,16,24,128]{3,2,1,0:T(8,128)S(1)}, ...), branch_computations={%region_0.0_spmd, %region_1.0_spmd, %region_2.0_spmd} | conditional | bytes 8 | solution.py:417
  8.6 62.1 %exchange_14.1 = f32[16,384,128]{2,1,0:T(8,128)} custom-call(s32[16,128]{1,0:T(8,128)S(1)} %get-tuple-element.38.table, f32[8,16,24,128]{3,2,1,0:T(8,128)S(1)} %get-tuple-element.39.send, f32[2,256,256]{2,1,0:T(8,128)} %get-tuple-element.40.pinv, f32[2,256,256]{2,1,0:T(8,128)} %get-tuple-element.41.ufac), custom_call_target="tpu_custom_call" | custom-call | tf_op jit(solution)/shard_map/cond/branch_1_fun/exchange_14/pallas_call | solution.py:356
  70.7 0.0 copy-done.1
  70.7 0.0 copy-done.3
  70.7 0.0 copy-done.5
  70.7 7.0 %assemble.1 = f32[2304,128]{1,0:T(8,128)} custom-call(s32[16,128]{1,0:T(8,128)S(1)} %get-tuple-element.49.table, s32[128]{0:T(128)S(1)} %copy-done.5, s32[4,128]{1,0:T(4,128)S(1)} %bitcast.10, f32[384,128]{1,0:T(8,128)S(1)} %broadcast_in_dim.8.mask, f32[2304,128]{1,0:T(8,128)S(1)} %bitcast.8, f32[256,24,128]{2,1,0:T(8,128)} %get-tuple-element.52.ret), custom_call_target="tpu_custom_call" | custom-call | tf_op jit(solution)/shard_map/assemble/pallas_call | solution.py:401
Async XLA Ops:
  0.8 1.3 %copy-start = (f32[1,6,49152]{2,0,1:T(1,128)S(1)}, f32[1,6,49152]{2,0,1:T(1,128)}, u32[]{:S(2)}) copy-start(f32[1,6,49152]{2,0,1:T(1,128)} %param.9) | copy-start | bytes 3538948
  2.1 0.7 copy-start.2
  2.8 0.7 copy-start.4
  8.5 62.2 %copy-start.1 = (f32[1,6,49152]{2,0,1:T(1,128)S(1)}, f32[1,6,49152]{2,0,1:T(1,128)}, u32[]{:S(2)}) copy-start(f32[1,6,49152]{2,0,1:T(1,128)} %param.9) | copy-start | bytes 3538948
  8.5 62.2 %copy-start.3 = (s32[128,4]{0,1:T(4,128)S(1)}, s32[128,4]{0,1:T(4,128)}, u32[]{:S(2)}) copy-start(s32[128,4]{0,1:T(4,128)} %param.11) | copy-start | bytes 6148
  8.5 62.2 %copy-start.5 = (s32[128]{0:T(128)S(1)}, s32[128]{0:T(128)}, u32[]{:S(2)}) copy-start(s32[128]{0:T(128)} %slots.3) | copy-start | bytes 1540

commit v3 on v2

v3 whole, which is shorter than its diff:
```python
import functools

import jax
import jax.numpy as jnp
from jax import lax
from jax.experimental import pallas as pl
from jax.experimental.pallas import tpu as pltpu
from jax.sharding import PartitionSpec as P

BLOCK = 128
PIV = 256
NX, NY, NZ = 4, 4, 8
PLANE = NX * NY
SLOT_DEV = 2
PAIRS = NZ
RING_SLOTS = NZ * SLOT_DEV
COLS = 6
ROW_BLOCKS = 384
MSG = COLS * 4
NEAR = 2
FAR = 6
PACKED = 768
MESH = pl.DeviceIdType.MESH
PEERS = (
    (0, 1), (1, 0), (0, 3), (3, 0), (1, 1), (3, 3), (1, 3), (3, 1),
    (0, 2), (2, 0), (1, 2), (2, 1), (3, 2), (2, 3), (2, 2),
)


def nt(a, b):
    return lax.dot_general(a, b, (((1,), (1,)), ((), ())), preferred_element_type=jnp.float32)


def nn(a, b):
    return lax.dot_general(a, b, (((1,), (0,)), ((), ())), preferred_element_type=jnp.float32)


def split(v):
    high = v.astype(jnp.bfloat16)
    low = (v - high.astype(jnp.float32)).astype(jnp.bfloat16)
    return high, low


def product(dot, x, w):
    xh, xl = split(x)
    wh, wl = split(w)
    both = dot(jnp.concatenate([xh, xl], axis=0), wh)
    n = x.shape[0]
    return both[:n] + (both[n:] + dot(xh, wl))


TIERS = (12, 14, 16)


def first_position(tier, o):
    p = o // 2
    last = o - 14 if p == PAIRS - 1 else 0
    if tier == 12:
        return (max(p - 1, 0) if p < 3 else 2 * p - 4) + last
    return max(2 * p - (16 - tier), 0) + last


def slot_in_sequence(o, z, ring):
    p, a = o >> 1, o & 1
    i = p - 1
    reach = (i >> 1) + 1
    edge = jnp.logical_or(p == 0, p == PAIRS - 1)
    zs = jnp.where(p == 0, z, jnp.where(a == 0, z - reach, z + reach)) & (NZ - 1)
    sl = jnp.where(edge, a, i & 1)
    zs = jnp.where(p == PAIRS - 1, z + NZ // 2, zs) & (NZ - 1)
    return (((ring >> 2) * NZ + zs) * NX + (ring & (NX - 1))) * SLOT_DEV + sl


def sequence_of(slot, z):
    sl = slot & 1
    ring = ((slot >> 6) << 2) + ((slot >> 1) & 3)
    delta = (z - (slot >> 3)) & (NZ - 1)
    below = delta < NZ // 2
    o = 4 * jnp.where(below, delta, NZ - delta) - 2 + 2 * sl + jnp.where(below, 0, 1)
    o = jnp.where(delta == NZ // 2, 2 * (PAIRS - 1) + sl, o)
    return jnp.where(delta == 0, sl, o), ring


def tables_kernel(slots_h, blocks_h, table, tier_ref, slots, blocks, sems):
    one = pltpu.make_async_copy(slots_h, slots, sems.at[0])
    two = pltpu.make_async_copy(blocks_h, blocks, sems.at[1])
    one.start()
    two.start()
    shape = (RING_SLOTS, 128)
    o_of = lax.broadcasted_iota(jnp.int32, shape, 0)
    lane = lax.broadcasted_iota(jnp.int32, shape, 1)
    slot_of = slot_in_sequence(o_of, lane >> 4, lane & 15)
    one.wait()
    two.wait()

    def mark(f, code):
        for k in range(8):
            g = 8 * f + k
            code = jnp.where(slot_of == slots[g], 1 + blocks[0, g] + (blocks[1, g] << 9), code)
        return code

    code = lax.fori_loop(0, slots.shape[0] // 8, mark, jnp.zeros(shape, jnp.int32))
    used = code > 0
    count = jnp.zeros((1, 128), jnp.int32)
    ranks = []
    last = {t: jnp.full((1, 128), -1, jnp.int32) for t in TIERS}
    places = {t: [] for t in TIERS}
    for o in range(RING_SLOTS):
        on = used[o : o + 1]
        ranks.append(jnp.where(on, count, 0))
        count = count + on.astype(jnp.int32)
        for t in TIERS:
            last[t] = jnp.where(on, jnp.maximum(last[t] + 1, first_position(t, o)), last[t])
            places[t].append(jnp.where(on, last[t], 255))
    fits = [jnp.max(last[t]) < t for t in TIERS]
    tier = jnp.where(fits[0], 0, jnp.where(fits[1], 1, 2))
    place = {t: jnp.concatenate(places[t], axis=0) for t in TIERS}
    place = jnp.where(tier == 0, place[TIERS[0]], jnp.where(tier == 1, place[TIERS[1]], place[TIERS[2]]))
    holds = jnp.zeros(shape, jnp.int32)
    by_rank = jnp.zeros(shape, jnp.int32)
    for o in range(RING_SLOTS):
        holds = jnp.where(place[o : o + 1] == o_of, o, holds)
        own = jnp.logical_and(used[o : o + 1], ranks[o] == o_of)
        by_rank = jnp.where(own, code[o : o + 1] - 1, by_rank)
    table[0:RING_SLOTS, :] = jnp.concatenate(ranks, axis=0) + (place << 8) + (holds << 16)
    table[RING_SLOTS : 2 * RING_SLOTS, :] = by_rank
    tier_ref[0] = tier


def make_tables(slots, blocks):
    hbm = pl.BlockSpec(memory_space=pltpu.HBM)
    return pl.pallas_call(
        tables_kernel,
        out_shape=(
            jax.ShapeDtypeStruct((2 * RING_SLOTS, 128), jnp.int32),
            jax.ShapeDtypeStruct((1,), jnp.int32),
        ),
        in_specs=[hbm, hbm],
        out_specs=(pl.BlockSpec(memory_space=pltpu.VMEM), pl.BlockSpec(memory_space=pltpu.SMEM)),
        scratch_shapes=[
            pltpu.SMEM(slots.shape, jnp.int32),
            pltpu.SMEM(blocks.shape, jnp.int32),
            pltpu.SemaphoreType.DMA((2,)),
        ],
        name="tables",
    )(slots, blocks)


def exchange_kernel(
    tier, table_h, pattern_h, rhs_h, pinv_h, ufac_h, ret, acc,
    table, pattern, rhs, pinv, ufac, mask, send, fac, near, arr, res, back, in_sems,
    ring_ss, ring_rs, core_ss, core_rs, out_ss, out_rs, ret_ss, ret_rs,
):
    r = lax.axis_index("rows")
    c = lax.axis_index("cols")
    x = lax.rem(r, NX)
    z = lax.rem(lax.div(r, NX), NZ)
    y = lax.div(r, NX * NZ)
    me = y * NX + x

    def chip(yy, zz, xx):
        return (yy * NZ + zz) * NX + xx

    def peer(dy, dx):
        return lax.rem(y + dy, NY), lax.rem(x + dx, NX)

    above = lax.rem(z + 1, NZ)
    below = lax.rem(z + NZ - 1, NZ)

    barrier = pltpu.get_barrier_semaphore()
    for dy, dx in PEERS:
        py, px = peer(dy, dx)
        pl.semaphore_signal(barrier, inc=1, device_id=(chip(py, z, px), c), device_id_type=MESH)
    for zz in (above, below):
        pl.semaphore_signal(barrier, inc=1, device_id=(chip(y, zz, x), c), device_id_type=MESH)
    pl.semaphore_signal(barrier, inc=1, device_id=(r, 1 - c), device_id_type=MESH)

    fetches = [
        pltpu.make_async_copy(src, dst, in_sems.at[k])
        for k, (src, dst) in enumerate(
            ((pinv_h, pinv), (ufac_h, ufac), (table_h, table), (pattern_h, pattern), (rhs_h, rhs))
        )
    ]
    for fetch in fetches:
        fetch.start()
    fetches[0].wait()
    fetches[1].wait()

    row = lax.broadcasted_iota(jnp.int32, (BLOCK, BLOCK), 0)
    col = lax.broadcasted_iota(jnp.int32, (BLOCK, BLOCK), 1)
    for s in range(SLOT_DEV):
        q = SLOT_DEV * z + s
        fac[q, 0:BLOCK, :] = jnp.where(
            row > col, pinv[s, :BLOCK, :BLOCK], pinv[s, BLOCK:, BLOCK:].T
        )
        fac[q, BLOCK : 2 * BLOCK, :] = pinv[s, BLOCK:, :BLOCK]
        fac[q, PIV : 2 * PIV, :] = ufac[s, :, :BLOCK]
        fac[q, 2 * PIV : 3 * PIV, :] = ufac[s, :, BLOCK:]

    pl.semaphore_wait(barrier, len(PEERS) + 3)

    half = pl.ds(pl.multiple_of(c * (PACKED // 2), PACKED // 2), PACKED // 2)

    def slot_at(i, d, away):
        zs = lax.rem(z - (1 - 2 * d) * (lax.div(i, 2) + away) + NZ, NZ)
        return SLOT_DEV * zs + lax.rem(i, 2)

    def slot_from(i, d):
        return slot_at(i, d, 1)

    def part(i, d):
        if i is not None and i >= FAR:
            at = c * (PACKED // 2) + d * (PACKED // 4)
            return pl.ds(pl.multiple_of(at, PACKED // 4), PACKED // 4)
        return half

    def ring_copy(i, d, far=None):
        q = slot_at(i, d, 0)
        view = fac.at[q, part(far, d), :]
        return pltpu.make_async_remote_copy(
            view, view, ring_ss.at[d, i], ring_rs.at[d, i],
            device_id=(chip(y, (above, below)[d], x), c), device_id_type=MESH,
        )

    def core_copy(i, d, far=None):
        view = fac.at[slot_from(i, d), part(far, d), :]
        return pltpu.make_async_remote_copy(
            view, view, core_ss.at[d, i], core_rs.at[d, i],
            device_id=(r, 1 - c), device_id_type=MESH,
        )

    lane = z * PLANE + me

    def pack(p):
        def one(m, carry):
            for a in range(2):
                code = table[RING_SLOTS + 2 * p + a, z * PLANE + m]
                for h, b in enumerate((code & 511, code >> 9)):
                    v = rhs[pl.ds(b, COLS, stride=ROW_BLOCKS), :] * mask[pl.ds(b, 1), :]
                    send[p, m, pl.ds(2 * a + h, COLS, stride=4), :] = v
            return carry

        lax.fori_loop(0, PLANE, one, 0, unroll=2)

    def rows_at(ref, p, m):
        return ref.at[p, pl.ds(pl.multiple_of(m * MSG, 8), MSG), :]

    def start_out(p, into):
        for dy, dx in PEERS:
            py, px = peer(dy, dx)
            pltpu.make_async_remote_copy(
                send.at[p, py * NX + px], rows_at(into, p, me), out_ss.at[p], out_rs.at[p],
                device_id=(chip(py, z, px), c), device_id_type=MESH,
            ).start()
        into[p, pl.ds(pl.multiple_of(me * MSG, 8), MSG), :] = send[p, me]

    def start_back(t):
        for dy, dx in PEERS:
            py, px = peer(dy, dx)
            pltpu.make_async_remote_copy(
                rows_at(back, t, py * NX + px), rows_at(ret, t, me), ret_ss.at[t], ret_rs.at[t],
                device_id=(chip(py, z, px), c), device_id_type=MESH,
            ).start()
        pltpu.make_async_copy(rows_at(back, t, me), rows_at(ret, t, me), ret_rs.at[t]).start()

    def wait_bytes(ref, p, n, sem):
        view = ref.at[p, pl.ds(0, n * MSG), :]
        pltpu.make_async_copy(view, view, sem).wait()

    def solve(o, q, data):
        k = table[o, lane] & 255
        data = data.at[k >> 1]
        second = (k & 1) == 1
        x0, x1 = (
            jnp.where(
                second,
                data[pl.ds(2 + h, PLANE * COLS, stride=4), :],
                data[pl.ds(h, PLANE * COLS, stride=4), :],
            )
            for h in range(2)
        )
        merged = fac[q, 0:BLOCK, :]
        lower = jnp.where(row > col, merged, 0.0)
        upper = jnp.where(row < col, merged, 0.0)
        left = jnp.concatenate([lower, fac[q, BLOCK:PIV, :]], axis=0)
        first = product(nt, x0, left)
        y0 = x0 + first[:, :BLOCK]
        y1 = x1 + (first[:, BLOCK:] + product(nn, x1, upper))
        upd = product(nt, y0, fac[q, PIV : 2 * PIV, :]) + product(nt, y1, fac[q, 2 * PIV : 3 * PIV, :])
        for h, v in enumerate((y0, y1, upd[:, :BLOCK], upd[:, BLOCK:])):
            res[o, pl.ds(h, PLANE * COLS, stride=4), :] = v

    def give_back(t):
        back[t] = res[table[t, lane] >> 16]
        start_back(t)

    for i in range(2):
        for d in range(2):
            ring_copy(jnp.int32(i), d).start()
    fetches[3].wait()
    for k in range(ROW_BLOCKS // BLOCK):
        on = pattern[:, k * BLOCK : (k + 1) * BLOCK].astype(jnp.float32)
        mask[k * BLOCK : (k + 1) * BLOCK, :] = jnp.broadcast_to(on, (BLOCK, BLOCK)).T
    fetches[2].wait()
    fetches[4].wait()
    for p in range(NEAR):
        pack(p)
        start_out(p, near)

    def out_step(p, carry):
        pack(p)
        start_out(p, arr)
        return carry

    lax.fori_loop(NEAR, tier // 2, out_step, 0)

    def init(k, carry):
        on = mask[pl.ds(pl.multiple_of(8 * k, 8), 8), :]
        for j in range(COLS):
            v = rhs[pl.ds(pl.multiple_of(j * ROW_BLOCKS + 8 * k, 8), 8), :] * on
            acc[pl.ds(64 * k + j, 8, stride=8), :] = v
        return carry

    lax.fori_loop(0, ROW_BLOCKS // 8, init, 0, unroll=2)

    for p in range(NEAR):
        wait_bytes(near, p, PLANE - 1, out_rs.at[p])
    for a in range(2):
        solve(a, SLOT_DEV * z + a, near)
    for t in range(first_position(tier, 2)):
        give_back(t)

    def advance(i):
        for d in range(2):
            ring_copy(i, d).wait_recv()

            @pl.when(i < FAR - 2)
            def _():
                ring_copy(i + 2, d).start()

            @pl.when(i >= FAR - 2)
            def _():
                ring_copy(i + 2, d, FAR).start()

            core_copy(i, d).start()
        for d in range(2):
            core_copy(i, d).wait_recv()

    advance(jnp.int32(0))
    for a in range(2):
        solve(2 + a, slot_from(jnp.int32(0), a), near)
    for t in range(first_position(tier, 2), first_position(tier, 4)):
        give_back(t)

    for p in range(NEAR):
        arr[p] = near[p]

    def arrive(p, carry):
        wait_bytes(arr, p, PLANE - 1, out_rs.at[p])
        return carry

    lax.fori_loop(NEAR, tier // 2, arrive, 0)

    def step(i, carry):
        advance(i)
        for a in range(2):
            solve(2 * i + 2 + a, slot_from(i, a), arr)
        p = i + 1
        if tier == 12:
            t = jnp.where(p < 3, p - 1, 2 * p - 4)
        else:
            t = 2 * p - (16 - tier)
        give_back(t)

        @pl.when(p >= (3 if tier == 12 else 0))
        def _():
            give_back(t + 1)

        return carry

    lax.fori_loop(1, FAR, step, 0)

    for i in range(FAR, FAR + 2):
        at = jnp.int32(i)
        for d in range(2):
            ring_copy(at, d, i).wait_recv()
            core_copy(at, d, i).start()
        for d in range(2):
            core_copy(at, d, i).wait_recv()
        solve(8 + i, slot_from(at, 0), arr)
        give_back(first_position(tier, 8 + i))

    def drain(i, carry):
        for d in range(2):
            ring_copy(i, d).wait_send()
            core_copy(i, d).wait_send()
        return carry

    lax.fori_loop(0, FAR, drain, 0)
    for i in range(FAR, FAR + 2):
        for d in range(2):
            ring_copy(jnp.int32(i), d, i).wait_send()
            core_copy(jnp.int32(i), d, i).wait_send()

    def drain_out(p, carry):
        wait_bytes(arr, p, PLANE - 1, out_ss.at[p])
        return carry

    lax.fori_loop(0, tier // 2, drain_out, 0)

    def drain_back(t, carry):
        wait_bytes(back, t, PLANE - 1, ret_ss.at[t])
        wait_bytes(back, t, PLANE, ret_rs.at[t])
        return carry

    lax.fori_loop(0, tier, drain_back, 0)


def exchange(tier, table, pattern, rhs, pinv, ufac):
    vmem = pl.BlockSpec(memory_space=pltpu.VMEM)
    hbm = pl.BlockSpec(memory_space=pl.ANY)
    dma = pltpu.SemaphoreType.DMA
    f32 = jnp.float32
    return pl.pallas_call(
        functools.partial(exchange_kernel, tier),
        out_shape=(
            jax.ShapeDtypeStruct((RING_SLOTS, PLANE * MSG, BLOCK), f32),
            jax.ShapeDtypeStruct((ROW_BLOCKS * 8, BLOCK), f32),
        ),
        in_specs=[hbm] * 5,
        out_specs=(hbm, vmem),
        scratch_shapes=[
            pltpu.SMEM(table.shape, jnp.int32),
            pltpu.VMEM(pattern.shape, jnp.int32),
            pltpu.VMEM(rhs.shape, f32),
            pltpu.VMEM(pinv.shape, f32),
            pltpu.VMEM(ufac.shape, f32),
            pltpu.VMEM((ROW_BLOCKS, BLOCK), f32),
            pltpu.VMEM((PAIRS, PLANE, MSG, BLOCK), f32),
            pltpu.VMEM((RING_SLOTS, PACKED, BLOCK), f32),
            pltpu.VMEM((NEAR, PLANE * MSG, BLOCK), f32),
            pltpu.VMEM((PAIRS, PLANE * MSG, BLOCK), f32),
            pltpu.VMEM((RING_SLOTS, PLANE * MSG, BLOCK), f32),
            pltpu.VMEM((RING_SLOTS, PLANE * MSG, BLOCK), f32),
            dma((5,)),
            dma((2, FAR + 2)), dma((2, FAR + 2)), dma((2, FAR + 2)), dma((2, FAR + 2)),
            dma((PAIRS,)), dma((PAIRS,)), dma((RING_SLOTS,)), dma((RING_SLOTS,)),
        ],
        compiler_params=pltpu.CompilerParams(
            collective_id=TIERS.index(tier), has_side_effects=True, vmem_limit_bytes=36 * 1024 * 1024
        ),
        name=f"exchange_{tier}",
    )(table, pattern, rhs, pinv, ufac)


def assemble_kernel(table, slots, blocks, ret, acc_in, out, acc, sems):
    z = lax.rem(lax.div(lax.axis_index("rows"), NX), NZ)
    acc[...] = acc_in[...]

    def one_front(f, carry):
        o, ring = sequence_of(slots[f], z)
        at = ((table[o, z * PLANE + ring] >> 8) & 255) * PLANE + ring
        for h in range(4):
            rows = pl.ds(pl.multiple_of(blocks[h, f] * 8, 8), COLS)
            v = ret[at, pl.ds(h, COLS, stride=4), :]
            acc[rows, :] = v if h < 2 else acc[rows, :] - v
        return carry

    lax.fori_loop(0, slots.shape[0], one_front, 0, unroll=4)

    def regroup(k, carry):
        for j in range(COLS):
            rows = pl.ds(pl.multiple_of(j * ROW_BLOCKS + 8 * k, 8), 8)
            out[rows, :] = acc[pl.ds(64 * k + j, 8, stride=8), :]
        return carry

    lax.fori_loop(0, ROW_BLOCKS // 8, regroup, 0, unroll=2)


def assemble(table, slots, blocks, ret, acc):
    vmem = pl.BlockSpec(memory_space=pltpu.VMEM)
    smem = pl.BlockSpec(memory_space=pltpu.SMEM)
    return pl.pallas_call(
        assemble_kernel,
        out_shape=jax.ShapeDtypeStruct((COLS * ROW_BLOCKS, BLOCK), jnp.float32),
        in_specs=[smem, smem, smem, vmem, vmem],
        out_specs=vmem,
        scratch_shapes=[pltpu.VMEM(acc.shape, jnp.float32), pltpu.SemaphoreType.DMA],
        compiler_params=pltpu.CompilerParams(vmem_limit_bytes=16 * 1024 * 1024),
        name="assemble",
    )(table, slots, blocks, ret, acc)


def branch(tier, table, slots, blocks, pattern, rhs, pinv, ufac):
    ret, acc = exchange(tier, table, pattern, rhs, pinv, ufac)
    return assemble(table, slots, blocks, ret.reshape(RING_SLOTS * PLANE, MSG, BLOCK), acc)


def on_device(rhs, pattern, front_blocks, front_slot, pivot_inverse, update_factor):
    shape = rhs.shape
    blocks = front_blocks.T
    table, tier = make_tables(front_slot, blocks)
    out = lax.switch(
        tier[0],
        [functools.partial(branch, t) for t in TIERS],
        table, front_slot, blocks, pattern.T, rhs.reshape(COLS * ROW_BLOCKS, BLOCK), pivot_inverse, update_factor,
    )
    return out.reshape(shape)


def solution(mesh):
    return jax.shard_map(
        on_device,
        mesh=mesh,
        in_specs=(
            P("cols", "rows", None),
            P(None, "cols"),
            P(),
            P(),
            P("rows", None, None),
            P("rows", None, None),
        ),
        out_specs=P("cols", "rows", None),
        check_vma=False,
    )
```

time: 76.9 us -> 66.2 us (0.86); the launches traced: 77.7 us -> 66 us
  Pallas kernels: 73.5 us -> 64.3 us
  local copies, waits for them, and re-layouts: 2.73 us -> 1.02 us
    pallas_call x3, Pallas kernels: 73.5 us -> 64.3 us  [the longest x1 58.6 us: exchange(): pl.pallas_call(functools.partial(exchange_kernel, tier), out_shape=(jax.S...]
    unnamed x12 -> x2, local copies, waits for them, and re-layouts: 2.62 us -> 1.01 us
where the time goes in v3:
time: 66.2 us; the launch traced here: 66 us
  Pallas kernels  64.3 us (97%)
  local copies, waits for them, and re-layouts  1.02 us (2%)
  between operations  0.67 us (1%)
    pallas_call x1, Pallas kernels, exchange(): pl.pallas_call(functools.partial(exchange_kernel, tier), out_shape=(jax.S...  58.6 us
    pallas_call x1, Pallas kernels, assemble(): pl.pallas_call(assemble_kernel, out_shape=jax.ShapeDtypeStruct((COLS * RO...  3.66 us
    pallas_call x1, Pallas kernels, make_tables(): pl.pallas_call(tables_kernel, out_shape=(jax.ShapeDtypeStruct((2 * RING_S...  1.98 us

profile of v3, /device:TPU:1, one launch (start us, length us, event | category | flops | bytes accessed | tf_op | source)
XLA Modules:
  0.0 66.0 jit_solution(9856700705560513224)
XLA Ops:
  0.0 2.0 %tables.1 = (s32[32,128]{1,0:T(8,128)S(1)}, s32[1]{0:T(128)}) custom-call(s32[128]{0:T(128)} %slots_h.1, s32[4,128]{1,0:T(4,128)} %bitcast.19), custom_call_target="tpu_custom_call" | custom-call | tf_op jit(solution)/shard_map/tables/pallas_call | solution.py:132
  2.6 62.4 %conditional.1 = (f32[1,6,49152]{2,0,1:T(1,128)S(1)}) conditional(s32[]{:T(128)} %bitcast.7, (s32[32,128]{1,0:T(8,128)S(1)}, s32[1,384]{1,0:T(1,128)}, f32[2304,128]{1,0:T(8,128)}, f32[2,256,256]{2,1,0:T(8,128)}, f32[2,256,256]{2,1,0:T(8,128)}, /*index=5*/s32[128]{0:T(128)}, s32[4,128]{1,0:T(4,128)}) %tuple.34, ...), branch_computations={%region_0.0_spmd, %region_1.0_spmd, %region_2.0_spmd} | conditional | bytes 10304 | solution.py:503
  2.6 0.0 copy-start.1
  2.7 0.0 copy-start.4
  2.7 58.6 %exchange_12.1 = (f32[16,384,128]{2,1,0:T(8,128)S(1)}, f32[3072,128]{1,0:T(8,128)S(1)}) custom-call(s32[32,128]{1,0:T(8,128)S(1)} %get-tuple-element.52.table_h.table, s32[1,384]{1,0:T(1,128)} %get-tuple-element.55.pattern_h, f32[2304,128]{1,0:T(8,128)} %get-tuple-element.56.rhs_h, f32[2,256,256]{2,1,0:T(8,128)} %get-tuple-element.57.pinv_h, ...), custom_call_target="tpu_custom_call" | custom-call | tf_op jit(solution)/shard_map/cond/branch_0_fun/exchange_12/pallas_call | solution.py:424
  61.3 0.0 copy-done.1
  61.3 0.0 copy-done.4
  61.3 3.7 %assemble.3 = f32[2304,128]{1,0:T(8,128)S(1)} custom-call(s32[32,128]{1,0:T(8,128)S(1)} %get-tuple-element.52.table_h.table, s32[128]{0:T(128)S(1)} %copy-done.4, s32[4,128]{1,0:T(4,128)S(1)} %copy-done.1, f32[256,24,128]{2,1,0:T(8,128)S(1)} %bitcast.10, f32[3072,128]{1,0:T(8,128)S(1)} %get-tuple-element.60.acc_in), custom_call_target="tpu_custom_call" | custom-call | tf_op jit(solution)/shard_map/cond/branch_0_fun/assemble/pallas_call | solution.py:483
  65.0 0.0 copy-start
  65.0 1.0 %copy-done = f32[1,6,49152]{2,0,1:T(1,128)} copy-done((f32[1,6,49152]{2,0,1:T(1,128)}, f32[1,6,49152]{2,0,1:T(1,128)S(1)}, u32[]{:S(2)}) %copy-start) | copy-done | bytes 1179672
Async XLA Ops:
  2.6 58.7 %copy-start.1 = (s32[4,128]{1,0:T(4,128)S(1)}, s32[4,128]{1,0:T(4,128)}, u32[]{:S(2)}) copy-start(s32[4,128]{1,0:T(4,128)} %get-tuple-element.54.blocks) | copy-start | bytes 6148 | tf_op jit(solution)/shard_map/cond
  2.7 58.7 %copy-start.4 = (s32[128]{0:T(128)S(1)}, s32[128]{0:T(128)}, u32[]{:S(2)}) copy-start(s32[128]{0:T(128)} %get-tuple-element.53.slots) | copy-start | bytes 1540 | tf_op jit(solution)/shard_map/cond
  65.0 1.0 %copy-start = (f32[1,6,49152]{2,0,1:T(1,128)}, f32[1,6,49152]{2,0,1:T(1,128)S(1)}, u32[]{:S(2)}) copy-start(f32[1,6,49152]{2,0,1:T(1,128)S(1)} %get-tuple-element.88) | copy-start | bytes 3538948

commit v4 on v3

v4 whole, which is shorter than its diff:
```python
import functools

import jax
import jax.numpy as jnp
from jax import lax
from jax.experimental import pallas as pl
from jax.experimental.pallas import tpu as pltpu
from jax.sharding import PartitionSpec as P

BLOCK = 128
PIV = 256
NX, NY, NZ = 4, 4, 8
PLANE = NX * NY
SLOT_DEV = 2
PAIRS = NZ
RING_SLOTS = NZ * SLOT_DEV
COLS = 6
ROW_BLOCKS = 384
MSG = COLS * 4
FAR = 6
PACKED = 768
MESH = pl.DeviceIdType.MESH
PEERS = (
    (2, 2), (2, 1), (2, 3), (1, 2), (3, 2), (1, 1), (3, 3), (1, 3),
    (3, 1), (0, 2), (2, 0), (0, 1), (1, 0), (0, 3), (3, 0),
)


def nt(a, b):
    return lax.dot_general(a, b, (((1,), (1,)), ((), ())), preferred_element_type=jnp.float32)


def nn(a, b):
    return lax.dot_general(a, b, (((1,), (0,)), ((), ())), preferred_element_type=jnp.float32)


def split(v):
    high = v.astype(jnp.bfloat16)
    low = (v - high.astype(jnp.float32)).astype(jnp.bfloat16)
    return high, low


def product(dot, x, w):
    xh, xl = split(x)
    wh, wl = split(w)
    both = dot(jnp.concatenate([xh, xl], axis=0), wh)
    n = x.shape[0]
    return both[:n] + (both[n:] + dot(xh, wl))


TIERS = (12, 14, 16)


def first_position(tier, o):
    p = o // 2
    last = o - 14 if p == PAIRS - 1 else 0
    if tier == 12:
        return (max(p - 1, 0) if p < 3 else 2 * p - 4) + last
    return max(2 * p - (16 - tier), 0) + last


def slot_in_sequence(o, z, ring):
    p, a = o >> 1, o & 1
    i = p - 1
    reach = (i >> 1) + 1
    edge = jnp.logical_or(p == 0, p == PAIRS - 1)
    zs = jnp.where(p == 0, z, jnp.where(a == 0, z - reach, z + reach)) & (NZ - 1)
    sl = jnp.where(edge, a, i & 1)
    zs = jnp.where(p == PAIRS - 1, z + NZ // 2, zs) & (NZ - 1)
    return (((ring >> 2) * NZ + zs) * NX + (ring & (NX - 1))) * SLOT_DEV + sl


def sequence_of(slot, z):
    sl = slot & 1
    ring = ((slot >> 6) << 2) + ((slot >> 1) & 3)
    delta = (z - (slot >> 3)) & (NZ - 1)
    below = delta < NZ // 2
    o = 4 * jnp.where(below, delta, NZ - delta) - 2 + 2 * sl + jnp.where(below, 0, 1)
    o = jnp.where(delta == NZ // 2, 2 * (PAIRS - 1) + sl, o)
    return jnp.where(delta == 0, sl, o), ring


def tables_kernel(slots_h, blocks_h, pinv_h, ufac_h, table, own, tier_ref, slots, blocks, pinv, ufac, sems):
    fetches = [
        pltpu.make_async_copy(src, dst, sems.at[k])
        for k, (src, dst) in enumerate(((slots_h, slots), (blocks_h, blocks), (pinv_h, pinv), (ufac_h, ufac)))
    ]
    for fetch in fetches:
        fetch.start()
    shape = (RING_SLOTS, 128)
    o_of = lax.broadcasted_iota(jnp.int32, shape, 0)
    lane = lax.broadcasted_iota(jnp.int32, shape, 1)
    slot_of = slot_in_sequence(o_of, lane >> 4, lane & 15)
    fetches[0].wait()
    fetches[1].wait()

    def mark(f, code):
        for k in range(8):
            g = 8 * f + k
            code = jnp.where(slot_of == slots[g], 1 + blocks[0, g] + (blocks[1, g] << 9), code)
        return code

    code = lax.fori_loop(0, slots.shape[0] // 8, mark, jnp.zeros(shape, jnp.int32))
    used = code > 0
    count = jnp.zeros((1, 128), jnp.int32)
    ranks = []
    last = {t: jnp.full((1, 128), -1, jnp.int32) for t in TIERS}
    places = {t: [] for t in TIERS}
    for o in range(RING_SLOTS):
        on = used[o : o + 1]
        ranks.append(jnp.where(on, count, 0))
        count = count + on.astype(jnp.int32)
        for t in TIERS:
            last[t] = jnp.where(on, jnp.maximum(last[t] + 1, first_position(t, o)), last[t])
            places[t].append(jnp.where(on, last[t], 255))
    fits = [jnp.max(last[t]) < t for t in TIERS]
    tier = jnp.where(fits[0], 0, jnp.where(fits[1], 1, 2))
    place = {t: jnp.concatenate(places[t], axis=0) for t in TIERS}
    place = jnp.where(tier == 0, place[TIERS[0]], jnp.where(tier == 1, place[TIERS[1]], place[TIERS[2]]))
    holds = jnp.zeros(shape, jnp.int32)
    by_rank = jnp.zeros(shape, jnp.int32)
    for o in range(RING_SLOTS):
        holds = jnp.where(place[o : o + 1] == o_of, o, holds)
        mine = jnp.logical_and(used[o : o + 1], ranks[o] == o_of)
        by_rank = jnp.where(mine, code[o : o + 1] - 1, by_rank)
    table[0:RING_SLOTS, :] = jnp.concatenate(ranks, axis=0) + (place << 8) + (holds << 16)
    table[RING_SLOTS : 2 * RING_SLOTS, :] = by_rank
    tier_ref[0] = tier
    fetches[2].wait()
    fetches[3].wait()

    row = lax.broadcasted_iota(jnp.int32, (BLOCK, BLOCK), 0)
    col = lax.broadcasted_iota(jnp.int32, (BLOCK, BLOCK), 1)
    for s in range(SLOT_DEV):
        own[s, 0:BLOCK, :] = jnp.where(
            row > col, pinv[s, :BLOCK, :BLOCK], pinv[s, BLOCK:, BLOCK:].T
        )
        own[s, BLOCK : 2 * BLOCK, :] = pinv[s, BLOCK:, :BLOCK]
        own[s, PIV : 2 * PIV, :] = ufac[s, :, :BLOCK]
        own[s, 2 * PIV : 3 * PIV, :] = ufac[s, :, BLOCK:]


def make_tables(slots, blocks, pinv, ufac):
    hbm = pl.BlockSpec(memory_space=pltpu.HBM)
    vmem = pl.BlockSpec(memory_space=pltpu.VMEM)
    return pl.pallas_call(
        tables_kernel,
        out_shape=(
            jax.ShapeDtypeStruct((2 * RING_SLOTS, 128), jnp.int32),
            jax.ShapeDtypeStruct((SLOT_DEV, PACKED, BLOCK), jnp.float32),
            jax.ShapeDtypeStruct((1,), jnp.int32),
        ),
        in_specs=[hbm] * 4,
        out_specs=(vmem, vmem, pl.BlockSpec(memory_space=pltpu.SMEM)),
        scratch_shapes=[
            pltpu.SMEM(slots.shape, jnp.int32),
            pltpu.SMEM(blocks.shape, jnp.int32),
            pltpu.VMEM(pinv.shape, jnp.float32),
            pltpu.VMEM(ufac.shape, jnp.float32),
            pltpu.SemaphoreType.DMA((4,)),
        ],
        compiler_params=pltpu.CompilerParams(vmem_limit_bytes=66_200_000),
        name="tables",
    )(slots, blocks, pinv, ufac)


def exchange_kernel(
    tier, own, table_h, slots_h, pattern_h, rhs_h, ret, acc, where,
    table, slots, pattern, rhs, mask, send, fac, land, arr, res, back, in_sems,
    ring_ss, ring_rs, core_ss, core_rs, out_ss, out_rs, ret_ss, ret_rs,
):
    r = lax.axis_index("rows")
    c = lax.axis_index("cols")
    x = lax.rem(r, NX)
    z = lax.rem(lax.div(r, NX), NZ)
    y = lax.div(r, NX * NZ)
    me = y * NX + x

    def chip(yy, zz, xx):
        return (yy * NZ + zz) * NX + xx

    def peer(dy, dx):
        return lax.rem(y + dy, NY), lax.rem(x + dx, NX)

    above = lax.rem(z + 1, NZ)
    below = lax.rem(z + NZ - 1, NZ)

    barrier = pltpu.get_barrier_semaphore()
    for dy, dx in PEERS:
        py, px = peer(dy, dx)
        pl.semaphore_signal(barrier, inc=1, device_id=(chip(py, z, px), c), device_id_type=MESH)
    for zz in (above, below):
        pl.semaphore_signal(barrier, inc=1, device_id=(chip(y, zz, x), c), device_id_type=MESH)
    pl.semaphore_signal(barrier, inc=1, device_id=(r, 1 - c), device_id_type=MESH)

    fetches = [
        pltpu.make_async_copy(src, dst, in_sems.at[k])
        for k, (src, dst) in enumerate(
            ((table_h, table), (pattern_h, pattern), (rhs_h, rhs), (slots_h, slots))
        )
    ]
    for fetch in fetches:
        fetch.start()
    pl.semaphore_wait(barrier, len(PEERS) + 3)

    def slot_at(i, d, away):
        zs = lax.rem(z - (1 - 2 * d) * (lax.div(i, 2) + away) + NZ, NZ)
        return SLOT_DEV * zs + lax.rem(i, 2)

    def slot_from(i, d):
        return slot_at(i, d, 1)

    def piece(k):
        at = (2 * c + k) * (PACKED // 4)
        return pl.ds(pl.multiple_of(at, PACKED // 4), PACKED // 4)

    def ring_copy(i, d, k, source=None):
        view = fac.at[slot_at(i, d, 0), piece(k), :]
        source = view if source is None else source.at[piece(k), :]
        return pltpu.make_async_remote_copy(
            source, view, ring_ss.at[d, k, i], ring_rs.at[d, k, i],
            device_id=(chip(y, (above, below)[d], x), c), device_id_type=MESH,
        )

    def core_copy(i, d, k):
        view = fac.at[slot_from(i, d), piece(k), :]
        return pltpu.make_async_remote_copy(
            view, view, core_ss.at[d, k, i], core_rs.at[d, k, i],
            device_id=(r, 1 - c), device_id_type=MESH,
        )

    pieces = tuple((k, d) for k in range(2) for d in range(2))
    far_pieces = ((0, 0), (1, 1))

    lane = z * PLANE + me

    def pack(p):
        def one(m, carry):
            for a in range(2):
                code = table[RING_SLOTS + 2 * p + a, z * PLANE + m]
                for h, b in enumerate((code & 511, code >> 9)):
                    v = rhs[pl.ds(b, COLS, stride=ROW_BLOCKS), :] * mask[pl.ds(b, 1), :]
                    send[p, m, pl.ds(2 * a + h, COLS, stride=4), :] = v
            return carry

        lax.fori_loop(0, PLANE, one, 0, unroll=2)

    def rows_at(ref, p, m):
        return ref.at[p, pl.ds(pl.multiple_of(m * MSG, 8), MSG), :]

    def start_out(p):
        for dy, dx in PEERS:
            py, px = peer(dy, dx)
            pltpu.make_async_remote_copy(
                send.at[p, py * NX + px], rows_at(land, p, me), out_ss.at[p], out_rs.at[p],
                device_id=(chip(py, z, px), c), device_id_type=MESH,
            ).start()
        land[p, pl.ds(pl.multiple_of(me * MSG, 8), MSG), :] = send[p, me]

    def start_back(t):
        for dy, dx in PEERS:
            py, px = peer(dy, dx)
            pltpu.make_async_remote_copy(
                rows_at(back, t, py * NX + px), rows_at(ret, t, me), ret_ss.at[t], ret_rs.at[t],
                device_id=(chip(py, z, px), c), device_id_type=MESH,
            ).start()
        pltpu.make_async_copy(rows_at(back, t, me), rows_at(ret, t, me), ret_rs.at[t]).start()

    def wait_bytes(ref, p, n, sem):
        view = ref.at[p, pl.ds(0, n * MSG), :]
        pltpu.make_async_copy(view, view, sem).wait()

    row = lax.broadcasted_iota(jnp.int32, (BLOCK, BLOCK), 0)
    col = lax.broadcasted_iota(jnp.int32, (BLOCK, BLOCK), 1)

    def solve(o, factor):
        k = table[o, lane] & 255
        data = arr.at[k >> 1]
        second = (k & 1) == 1
        x0, x1 = (
            jnp.where(
                second,
                data[pl.ds(2 + h, PLANE * COLS, stride=4), :],
                data[pl.ds(h, PLANE * COLS, stride=4), :],
            )
            for h in range(2)
        )
        merged = factor[0:BLOCK, :]
        lower = jnp.where(row > col, merged, 0.0)
        upper = jnp.where(row < col, merged, 0.0)
        left = jnp.concatenate([lower, factor[BLOCK:PIV, :]], axis=0)
        first = product(nt, x0, left)
        y0 = x0 + first[:, :BLOCK]
        y1 = x1 + (first[:, BLOCK:] + product(nn, x1, upper))
        upd = product(nt, y0, factor[PIV : 2 * PIV, :]) + product(nt, y1, factor[2 * PIV : 3 * PIV, :])
        for h, v in enumerate((y0, y1, upd[:, :BLOCK], upd[:, BLOCK:])):
            res[o, pl.ds(h, PLANE * COLS, stride=4), :] = v

    def give_back(t):
        back[t] = res[table[t, lane] >> 16]
        start_back(t)

    for i in range(SLOT_DEV):
        for k, d in pieces:
            ring_copy(jnp.int32(i), d, k, own.at[i]).start()
    fetches[1].wait()
    for k in range(ROW_BLOCKS // BLOCK):
        on = pattern[:, k * BLOCK : (k + 1) * BLOCK].astype(jnp.float32)
        mask[k * BLOCK : (k + 1) * BLOCK, :] = jnp.broadcast_to(on, (BLOCK, BLOCK)).T
    fetches[0].wait()
    fetches[2].wait()

    def out_step(p, carry):
        pack(p)
        start_out(p)
        return carry

    lax.fori_loop(0, tier // 2, out_step, 0)

    def init(k, carry):
        on = mask[pl.ds(pl.multiple_of(8 * k, 8), 8), :]
        for j in range(COLS):
            v = rhs[pl.ds(pl.multiple_of(j * ROW_BLOCKS + 8 * k, 8), 8), :] * on
            acc[pl.ds(64 * k + j, 8, stride=8), :] = v
        return carry

    lax.fori_loop(0, ROW_BLOCKS // 8, init, 0, unroll=2)
    fetches[3].wait()

    def locate(f, carry):
        o, ring = sequence_of(slots[f], z)
        where[f] = ((table[o, z * PLANE + ring] >> 8) & 255) * PLANE + ring
        return carry

    lax.fori_loop(0, slots.shape[0], locate, 0, unroll=8)

    def forward(i):
        for k, d in pieces:
            ring_copy(i, d, k).wait_recv()

            @pl.when(i < (FAR if k == d else FAR - 2))
            def _():
                ring_copy(i + 2, d, k).start()

            core_copy(i, d, k).start()

    def collect(i):
        for k, d in pieces:
            core_copy(i, d, k).wait_recv()

    def arrive(p):
        wait_bytes(land, p, PLANE - 1, out_rs.at[p])
        arr[p] = land[p]

    zero = jnp.int32(0)
    forward(zero)
    arrive(0)
    for a in range(2):
        solve(a, own.at[a])
    for t in range(first_position(tier, 2)):
        give_back(t)
    arrive(1)
    collect(zero)
    for a in range(2):
        solve(2 + a, fac.at[slot_from(zero, a)])
    for t in range(first_position(tier, 2), first_position(tier, 4)):
        give_back(t)

    def step(i, carry):
        forward(i)

        @pl.when(i + 1 < tier // 2)
        def _():
            arrive(i + 1)

        collect(i)
        for a in range(2):
            solve(2 * i + 2 + a, fac.at[slot_from(i, a)])
        p = i + 1
        if tier == 12:
            t = jnp.where(p < 3, p - 1, 2 * p - 4)
        else:
            t = 2 * p - (16 - tier)
        give_back(t)

        @pl.when(p >= (3 if tier == 12 else 0))
        def _():
            give_back(t + 1)

        return carry

    lax.fori_loop(1, FAR, step, 0)

    if tier == 2 * PAIRS:
        arrive(PAIRS - 1)
    for i in range(FAR, FAR + 2):
        at = jnp.int32(i)
        for k, d in far_pieces:
            ring_copy(at, d, k).wait_recv()
            core_copy(at, d, k).start()
        for k, d in far_pieces:
            core_copy(at, d, k).wait_recv()
        solve(8 + i, fac.at[slot_from(at, 0)])
        give_back(first_position(tier, 8 + i))

    def drain(i, carry):
        for k, d in pieces:
            ring_copy(i, d, k).wait_send()
            core_copy(i, d, k).wait_send()
        return carry

    lax.fori_loop(0, FAR, drain, 0)
    for i in range(FAR, FAR + 2):
        for k, d in far_pieces:
            ring_copy(jnp.int32(i), d, k).wait_send()
            core_copy(jnp.int32(i), d, k).wait_send()

    def drain_out(p, carry):
        wait_bytes(arr, p, PLANE - 1, out_ss.at[p])
        return carry

    lax.fori_loop(0, tier // 2, drain_out, 0)

    def drain_back(t, carry):
        wait_bytes(back, t, PLANE - 1, ret_ss.at[t])
        wait_bytes(back, t, PLANE, ret_rs.at[t])
        return carry

    lax.fori_loop(0, tier, drain_back, 0)


def exchange(tier, own, table, slots, pattern, rhs):
    vmem = pl.BlockSpec(memory_space=pltpu.VMEM)
    hbm = pl.BlockSpec(memory_space=pl.ANY)
    dma = pltpu.SemaphoreType.DMA
    f32 = jnp.float32
    return pl.pallas_call(
        functools.partial(exchange_kernel, tier),
        out_shape=(
            jax.ShapeDtypeStruct((RING_SLOTS, PLANE * MSG, BLOCK), f32),
            jax.ShapeDtypeStruct((ROW_BLOCKS * 8, BLOCK), f32),
            jax.ShapeDtypeStruct(slots.shape, jnp.int32),
        ),
        in_specs=[vmem] + [hbm] * 4,
        out_specs=(hbm, vmem, pl.BlockSpec(memory_space=pltpu.SMEM)),
        scratch_shapes=[
            pltpu.SMEM(table.shape, jnp.int32),
            pltpu.SMEM(slots.shape, jnp.int32),
            pltpu.VMEM(pattern.shape, jnp.int32),
            pltpu.VMEM(rhs.shape, f32),
            pltpu.VMEM((ROW_BLOCKS, BLOCK), f32),
            pltpu.VMEM((PAIRS, PLANE, MSG, BLOCK), f32),
            pltpu.VMEM((RING_SLOTS, PACKED, BLOCK), f32),
            pltpu.VMEM((PAIRS, PLANE * MSG, BLOCK), f32),
            pltpu.VMEM((PAIRS, PLANE * MSG, BLOCK), f32),
            pltpu.VMEM((RING_SLOTS, PLANE * MSG, BLOCK), f32),
            pltpu.VMEM((RING_SLOTS, PLANE * MSG, BLOCK), f32),
            dma((4,)),
            *[dma((2, 2, FAR + 2))] * 4,
            dma((PAIRS,)), dma((PAIRS,)), dma((RING_SLOTS,)), dma((RING_SLOTS,)),
        ],
        compiler_params=pltpu.CompilerParams(
            collective_id=TIERS.index(tier), has_side_effects=True, vmem_limit_bytes=36 * 1024 * 1024
        ),
        name=f"exchange_{tier}",
    )(own, table, slots, pattern, rhs)


def assemble_kernel(where, blocks, ret, acc_in, out_h, acc, out, sems):
    del acc_in

    def one_front(f, carry):
        at = where[f]
        for h in range(4):
            rows = pl.ds(pl.multiple_of(blocks[h, f] * 8, 8), COLS)
            v = ret[at, pl.ds(h, COLS, stride=4), :]
            acc[rows, :] = v if h < 2 else acc[rows, :] - v
        return carry

    lax.fori_loop(0, where.shape[0], one_front, 0, unroll=8)

    copies = []
    for j in range(COLS):

        def regroup(k, carry):
            rows = pl.ds(pl.multiple_of(j * ROW_BLOCKS + 8 * k, 8), 8)
            out[rows, :] = acc[pl.ds(64 * k + j, 8, stride=8), :]
            return carry

        lax.fori_loop(0, ROW_BLOCKS // 8, regroup, 0, unroll=8)
        rows = pl.ds(j * ROW_BLOCKS, ROW_BLOCKS)
        copies.append(pltpu.make_async_copy(out.at[rows, :], out_h.at[rows, :], sems.at[j]))
        copies[-1].start()
    for copy in copies:
        copy.wait()


def assemble(where, blocks, ret, acc):
    vmem = pl.BlockSpec(memory_space=pltpu.VMEM)
    smem = pl.BlockSpec(memory_space=pltpu.SMEM)
    shape = (COLS * ROW_BLOCKS, BLOCK)
    return pl.pallas_call(
        assemble_kernel,
        out_shape=(
            jax.ShapeDtypeStruct(shape, jnp.float32),
            jax.ShapeDtypeStruct(acc.shape, jnp.float32),
        ),
        in_specs=[smem, smem, vmem, vmem],
        out_specs=(pl.BlockSpec(memory_space=pltpu.HBM), vmem),
        scratch_shapes=[pltpu.VMEM(shape, jnp.float32), pltpu.SemaphoreType.DMA((COLS,))],
        input_output_aliases={3: 1},
        compiler_params=pltpu.CompilerParams(vmem_limit_bytes=16 * 1024 * 1024),
        name="assemble",
    )(where, blocks, ret, acc)[0]


def branch(tier, own, table, slots, blocks, pattern, rhs):
    ret, acc, where = exchange(tier, own, table, slots, pattern, rhs)
    return assemble(where, blocks, ret.reshape(RING_SLOTS * PLANE, MSG, BLOCK), acc)


def on_device(rhs, pattern, front_blocks, front_slot, pivot_inverse, update_factor):
    shape = rhs.shape
    blocks = front_blocks.T
    table, own, tier = make_tables(front_slot, blocks, pivot_inverse, update_factor)
    out = lax.switch(
        tier[0],
        [functools.partial(branch, t) for t in TIERS],
        own, table, front_slot, blocks, pattern.T, rhs.reshape(COLS * ROW_BLOCKS, BLOCK),
    )
    return out.reshape(shape)


def solution(mesh):
    return jax.shard_map(
        on_device,
        mesh=mesh,
        in_specs=(
            P("cols", "rows", None),
            P(None, "cols"),
            P(),
            P(),
            P("rows", None, None),
            P("rows", None, None),
        ),
        out_specs=P("cols", "rows", None),
        check_vma=False,
    )
```

time: 66.2 us -> 59.5 us (0.90)
  Pallas kernels: 64.3 us -> 58.7 us
  local copies, waits for them, and re-layouts: 1.02 us -> 0.01 us
    pallas_call x1, Pallas kernels: 58.6 us -> 53.6 us  [exchange(): pl.pallas_call(functools.partial(exchange_kernel, tier), out_shape=(jax.S...]
    unnamed x2 -> x0, local copies, waits for them, and re-layouts: 1.01 us -> none
where the time goes in v4:
time: 59.5 us; the launch traced here: 59.4 us
  Pallas kernels  58.7 us (99%)
  between operations  0.66 us (1%)
    pallas_call x1, Pallas kernels, exchange(): pl.pallas_call(functools.partial(exchange_kernel, tier), out_shape=(jax.S...  53.6 us
    pallas_call x1, Pallas kernels, assemble(): pl.pallas_call(assemble_kernel, out_shape=(jax.ShapeDtypeStruct(shape, jn...  3.05 us
    pallas_call x1, Pallas kernels, make_tables(): pl.pallas_call(tables_kernel, out_shape=(jax.ShapeDtypeStruct((2 * RING_S...  2.01 us

profile of v4, /device:TPU:1, one launch (start us, length us, event | category | flops | bytes accessed | tf_op | source)
XLA Modules:
  0.0 59.4 jit_solution(1697682541082737485)
XLA Ops:
  0.0 2.0 %tables.1 = (s32[32,128]{1,0:T(8,128)S(1)}, f32[2,768,128]{2,1,0:T(8,128)S(1)}, s32[1]{0:T(128)}) custom-call(s32[128]{0:T(128)} %slots_h.1, s32[4,128]{1,0:T(4,128)} %bitcast.16, f32[2,256,256]{2,1,0:T(8,128)} %pinv_h.1, f32[2,256,256]{2,1,0:T(8,128)} %ufac_h.1), custom_call_target="tpu_custom_call" | custom-call | tf_op jit(solution)/shard_map/tables/pallas_call | solution.py:146
  2.7 56.7 %conditional.1 = (f32[1,6,49152]{2,0,1:T(1,128)}) conditional(s32[]{:T(128)} %bitcast.7, (f32[2,768,128]{2,1,0:T(8,128)S(1)}, s32[32,128]{1,0:T(8,128)S(1)}, s32[128]{0:T(128)}, s32[1,384]{1,0:T(1,128)}, f32[2304,128]{1,0:T(8,128)}, /*index=5*/s32[4,128]{1,0:T(4,128)}) %tuple.30, (f32[2,768,128]{2,1,0:T(8,128)S(1)}, ...), branch_computations={%region_0.0_spmd, %region_1.0_spmd, %region_2.0_spmd} | conditional | bytes 8228 | solution.py:526
  2.7 0.0 copy-start
  2.7 53.6 %exchange_12.1 = (f32[16,384,128]{2,1,0:T(8,128)S(1)}, f32[3072,128]{1,0:T(8,128)S(1)}, s32[128]{0:T(128)S(1)}) custom-call(f32[2,768,128]{2,1,0:T(8,128)S(1)} %get-tuple-element.44.own, s32[32,128]{1,0:T(8,128)S(1)} %get-tuple-element.46.table_h, s32[128]{0:T(128)} %get-tuple-element.47.slots_h, s32[1,384]{1,0:T(1,128)} %get-tuple-element.48.pattern_h, ...), custom_call_target="tpu_custom_call" | custom-call | tf_op jit(solution)/shard_map/cond/branch_0_fun/exchange_12/pallas_call | solution.py:437
  56.3 0.0 copy-done
  56.3 3.1 %assemble.3 = (f32[2304,128]{1,0:T(8,128)}, f32[3072,128]{1,0:T(8,128)S(1)}) custom-call(s32[128]{0:T(128)S(1)} %get-tuple-element.50.where, s32[4,128]{1,0:T(4,128)S(1)} %copy-done, f32[256,24,128]{2,1,0:T(8,128)S(1)} %bitcast.10, f32[3072,128]{1,0:T(8,128)S(1)} %get-tuple-element.53.acc_in), custom_call_target="tpu_custom_call", output_to_operand_aliasing={{1}: (3, {})} | custom-call | tf_op jit(solution)/shard_map/cond/branch_0_fun/assemble/pallas_call | solution.py:502
Async XLA Ops:
  2.7 53.6 %copy-start = (s32[4,128]{1,0:T(4,128)S(1)}, s32[4,128]{1,0:T(4,128)}, u32[]{:S(2)}) copy-start(s32[4,128]{1,0:T(4,128)} %get-tuple-element.51.blocks) | copy-start | bytes 6148 | tf_op jit(solution)/shard_map/cond

commit v5 on v4

--- a/solution.py
+++ b/solution.py
@@ -52,11 +52,10 @@
 
 
 def first_position(tier, o):
-    p = o // 2
-    last = o - 14 if p == PAIRS - 1 else 0
+    p, a = o // 2, o % 2
     if tier == 12:
-        return (max(p - 1, 0) if p < 3 else 2 * p - 4) + last
-    return max(2 * p - (16 - tier), 0) + last
+        return max(p - 1, 0) if p < 3 else 2 * p - 4 + a
+    return max(2 * p - (16 - tier) + a, 0) if p else a * (tier == 16)
 
 
 def slot_in_sequence(o, z, ring):
@@ -64,7 +63,8 @@
     i = p - 1
     reach = (i >> 1) + 1
     edge = jnp.logical_or(p == 0, p == PAIRS - 1)
-    zs = jnp.where(p == 0, z, jnp.where(a == 0, z - reach, z + reach)) & (NZ - 1)
+    lower = (a ^ jnp.where(z < NZ // 2, 1, 0)) == 0
+    zs = jnp.where(p == 0, z, jnp.where(lower, z - reach, z + reach)) & (NZ - 1)
     sl = jnp.where(edge, a, i & 1)
     zs = jnp.where(p == PAIRS - 1, z + NZ // 2, zs) & (NZ - 1)
     return (((ring >> 2) * NZ + zs) * NX + (ring & (NX - 1))) * SLOT_DEV + sl
@@ -75,15 +75,16 @@
     ring = ((slot >> 6) << 2) + ((slot >> 1) & 3)
     delta = (z - (slot >> 3)) & (NZ - 1)
     below = delta < NZ // 2
-    o = 4 * jnp.where(below, delta, NZ - delta) - 2 + 2 * sl + jnp.where(below, 0, 1)
+    o = 4 * jnp.where(below, delta, NZ - delta) - 2 + 2 * sl
+    o = o + (jnp.where(below, 0, 1) ^ jnp.where(z < NZ // 2, 1, 0))
     o = jnp.where(delta == NZ // 2, 2 * (PAIRS - 1) + sl, o)
     return jnp.where(delta == 0, sl, o), ring
 
 
-def tables_kernel(slots_h, blocks_h, pinv_h, ufac_h, table, own, tier_ref, slots, blocks, pinv, ufac, sems):
+def tables_kernel(slots_h, pinv_h, ufac_h, table, own, tier_ref, slots, pinv, ufac, sems):
     fetches = [
         pltpu.make_async_copy(src, dst, sems.at[k])
-        for k, (src, dst) in enumerate(((slots_h, slots), (blocks_h, blocks), (pinv_h, pinv), (ufac_h, ufac)))
+        for k, (src, dst) in enumerate(((slots_h, slots), (pinv_h, pinv), (ufac_h, ufac)))
     ]
     for fetch in fetches:
         fetch.start()
@@ -92,15 +93,14 @@
     lane = lax.broadcasted_iota(jnp.int32, shape, 1)
     slot_of = slot_in_sequence(o_of, lane >> 4, lane & 15)
     fetches[0].wait()
-    fetches[1].wait()
 
     def mark(f, code):
-        for k in range(8):
-            g = 8 * f + k
-            code = jnp.where(slot_of == slots[g], 1 + blocks[0, g] + (blocks[1, g] << 9), code)
+        for k in range(16):
+            g = 16 * f + k
+            code = jnp.where(slot_of == slots[g], 1 + g, code)
         return code
 
-    code = lax.fori_loop(0, slots.shape[0] // 8, mark, jnp.zeros(shape, jnp.int32))
+    code = lax.fori_loop(0, slots.shape[0] // 16, mark, jnp.zeros(shape, jnp.int32))
     used = code > 0
     count = jnp.zeros((1, 128), jnp.int32)
     ranks = []
@@ -126,8 +126,8 @@
     table[0:RING_SLOTS, :] = jnp.concatenate(ranks, axis=0) + (place << 8) + (holds << 16)
     table[RING_SLOTS : 2 * RING_SLOTS, :] = by_rank
     tier_ref[0] = tier
+    fetches[1].wait()
     fetches[2].wait()
-    fetches[3].wait()
 
     row = lax.broadcasted_iota(jnp.int32, (BLOCK, BLOCK), 0)
     col = lax.broadcasted_iota(jnp.int32, (BLOCK, BLOCK), 1)
@@ -140,7 +140,7 @@
         own[s, 2 * PIV : 3 * PIV, :] = ufac[s, :, BLOCK:]
 
 
-def make_tables(slots, blocks, pinv, ufac):
+def make_tables(slots, pinv, ufac):
     hbm = pl.BlockSpec(memory_space=pltpu.HBM)
     vmem = pl.BlockSpec(memory_space=pltpu.VMEM)
     return pl.pallas_call(
@@ -150,23 +150,22 @@
             jax.ShapeDtypeStruct((SLOT_DEV, PACKED, BLOCK), jnp.float32),
             jax.ShapeDtypeStruct((1,), jnp.int32),
         ),
-        in_specs=[hbm] * 4,
+        in_specs=[hbm] * 3,
         out_specs=(vmem, vmem, pl.BlockSpec(memory_space=pltpu.SMEM)),
         scratch_shapes=[
             pltpu.SMEM(slots.shape, jnp.int32),
-            pltpu.SMEM(blocks.shape, jnp.int32),
             pltpu.VMEM(pinv.shape, jnp.float32),
             pltpu.VMEM(ufac.shape, jnp.float32),
-            pltpu.SemaphoreType.DMA((4,)),
+            pltpu.SemaphoreType.DMA((3,)),
         ],
         compiler_params=pltpu.CompilerParams(vmem_limit_bytes=66_200_000),
         name="tables",
-    )(slots, blocks, pinv, ufac)
+    )(slots, pinv, ufac)
 
 
 def exchange_kernel(
-    tier, own, table_h, slots_h, pattern_h, rhs_h, ret, acc, where,
-    table, slots, pattern, rhs, mask, send, fac, land, arr, res, back, in_sems,
+    tier, own, table_h, slots_h, blocks_h, pattern_h, rhs_h, ret, acc, where,
+    table, slots, blocks, pattern, rhs, mask, send, fac, land, arr, res, back, in_sems,
     ring_ss, ring_rs, core_ss, core_rs, out_ss, out_rs, ret_ss, ret_rs,
 ):
     r = lax.axis_index("rows")
@@ -196,7 +195,7 @@
     fetches = [
         pltpu.make_async_copy(src, dst, in_sems.at[k])
         for k, (src, dst) in enumerate(
-            ((table_h, table), (pattern_h, pattern), (rhs_h, rhs), (slots_h, slots))
+            ((table_h, table), (pattern_h, pattern), (rhs_h, rhs), (slots_h, slots), (blocks_h, blocks))
         )
     ]
     for fetch in fetches:
@@ -219,7 +218,7 @@
         source = view if source is None else source.at[piece(k), :]
         return pltpu.make_async_remote_copy(
             source, view, ring_ss.at[d, k, i], ring_rs.at[d, k, i],
-            device_id=(chip(y, (above, below)[d], x), c), device_id_type=MESH,
+            device_id=(chip(y, jnp.where(d == 0, above, below), x), c), device_id_type=MESH,
         )
 
     def core_copy(i, d, k):
@@ -237,8 +236,9 @@
     def pack(p):
         def one(m, carry):
             for a in range(2):
-                code = table[RING_SLOTS + 2 * p + a, z * PLANE + m]
-                for h, b in enumerate((code & 511, code >> 9)):
+                f = table[RING_SLOTS + 2 * p + a, z * PLANE + m]
+                for h in range(2):
+                    b = blocks[h, f]
                     v = rhs[pl.ds(b, COLS, stride=ROW_BLOCKS), :] * mask[pl.ds(b, 1), :]
                     send[p, m, pl.ds(2 * a + h, COLS, stride=4), :] = v
             return carry
@@ -308,6 +308,7 @@
         on = pattern[:, k * BLOCK : (k + 1) * BLOCK].astype(jnp.float32)
         mask[k * BLOCK : (k + 1) * BLOCK, :] = jnp.broadcast_to(on, (BLOCK, BLOCK)).T
     fetches[0].wait()
+    fetches[4].wait()
     fetches[2].wait()
 
     def out_step(p, carry):
@@ -327,25 +328,31 @@
     lax.fori_loop(0, ROW_BLOCKS // 8, init, 0, unroll=2)
     fetches[3].wait()
 
+    fronts = slots.shape[0]
+
     def locate(f, carry):
         o, ring = sequence_of(slots[f], z)
-        where[f] = ((table[o, z * PLANE + ring] >> 8) & 255) * PLANE + ring
-        return carry
-
-    lax.fori_loop(0, slots.shape[0], locate, 0, unroll=8)
-
-    def forward(i):
-        for k, d in pieces:
+        where[f] = (((table[o, z * PLANE + ring] >> 8) & 255) * PLANE + ring) * MSG
+        for h in range(4):
+            where[(h + 1) * fronts + f] = blocks[h, f] * 8
+        return carry
+
+    lax.fori_loop(0, fronts, locate, 0, unroll=4)
+
+    early = jnp.where(z < NZ // 2, 1, 0)
+
+    def forward(i, d):
+        for k in range(2):
             ring_copy(i, d, k).wait_recv()
 
-            @pl.when(i < (FAR if k == d else FAR - 2))
+            @pl.when(i < jnp.where(d == k, FAR, FAR - 2))
             def _():
                 ring_copy(i + 2, d, k).start()
 
             core_copy(i, d, k).start()
 
-    def collect(i):
-        for k, d in pieces:
+    def collect(i, d):
+        for k in range(2):
             core_copy(i, d, k).wait_recv()
 
     def arrive(p):
@@ -353,40 +360,42 @@
         arr[p] = land[p]
 
     zero = jnp.int32(0)
-    forward(zero)
+    forward(zero, early)
+    forward(zero, 1 - early)
     arrive(0)
     for a in range(2):
         solve(a, own.at[a])
     for t in range(first_position(tier, 2)):
         give_back(t)
     arrive(1)
-    collect(zero)
-    for a in range(2):
-        solve(2 + a, fac.at[slot_from(zero, a)])
+    for a, d in enumerate((early, 1 - early)):
+        collect(zero, d)
+        solve(2 + a, fac.at[slot_from(zero, d)])
     for t in range(first_position(tier, 2), first_position(tier, 4)):
         give_back(t)
 
     def step(i, carry):
-        forward(i)
-
-        @pl.when(i + 1 < tier // 2)
-        def _():
-            arrive(i + 1)
-
-        collect(i)
-        for a in range(2):
-            solve(2 * i + 2 + a, fac.at[slot_from(i, a)])
         p = i + 1
-        if tier == 12:
-            t = jnp.where(p < 3, p - 1, 2 * p - 4)
-        else:
-            t = 2 * p - (16 - tier)
-        give_back(t)
-
-        @pl.when(p >= (3 if tier == 12 else 0))
-        def _():
-            give_back(t + 1)
-
+        for a, d in enumerate((early, 1 - early)):
+            forward(i, d)
+            if a == 0:
+
+                @pl.when(p < tier // 2)
+                def _():
+                    arrive(p)
+
+            collect(i, d)
+            solve(2 * p + a, fac.at[slot_from(i, d)])
+            if tier != 12:
+                give_back(2 * p - (16 - tier) + a)
+            elif a == 0:
+
+                @pl.when(p >= 3)
+                def _():
+                    give_back(2 * p - 4)
+
+            else:
+                give_back(jnp.where(p < 3, p - 1, 2 * p - 3))
         return carry
 
     lax.fori_loop(1, FAR, step, 0)
@@ -429,7 +438,7 @@
     lax.fori_loop(0, tier, drain_back, 0)
 
 
-def exchange(tier, own, table, slots, pattern, rhs):
+def exchange(tier, own, table, slots, blocks, pattern, rhs):
     vmem = pl.BlockSpec(memory_space=pltpu.VMEM)
     hbm = pl.BlockSpec(memory_space=pl.ANY)
     dma = pltpu.SemaphoreType.DMA
@@ -439,13 +448,14 @@
         out_shape=(
             jax.ShapeDtypeStruct((RING_SLOTS, PLANE * MSG, BLOCK), f32),
             jax.ShapeDtypeStruct((ROW_BLOCKS * 8, BLOCK), f32),
-            jax.ShapeDtypeStruct(slots.shape, jnp.int32),
+            jax.ShapeDtypeStruct((5 * slots.shape[0],), jnp.int32),
         ),
-        in_specs=[vmem] + [hbm] * 4,
+        in_specs=[vmem] + [hbm] * 5,
         out_specs=(hbm, vmem, pl.BlockSpec(memory_space=pltpu.SMEM)),
         scratch_shapes=[
             pltpu.SMEM(table.shape, jnp.int32),
             pltpu.SMEM(slots.shape, jnp.int32),
+            pltpu.SMEM(blocks.shape, jnp.int32),
             pltpu.VMEM(pattern.shape, jnp.int32),
             pltpu.VMEM(rhs.shape, f32),
             pltpu.VMEM((ROW_BLOCKS, BLOCK), f32),
@@ -455,7 +465,7 @@
             pltpu.VMEM((PAIRS, PLANE * MSG, BLOCK), f32),
             pltpu.VMEM((RING_SLOTS, PLANE * MSG, BLOCK), f32),
             pltpu.VMEM((RING_SLOTS, PLANE * MSG, BLOCK), f32),
-            dma((4,)),
+            dma((5,)),
             *[dma((2, 2, FAR + 2))] * 4,
             dma((PAIRS,)), dma((PAIRS,)), dma((RING_SLOTS,)), dma((RING_SLOTS,)),
         ],
@@ -463,21 +473,22 @@
             collective_id=TIERS.index(tier), has_side_effects=True, vmem_limit_bytes=36 * 1024 * 1024
         ),
         name=f"exchange_{tier}",
-    )(own, table, slots, pattern, rhs)
-
-
-def assemble_kernel(where, blocks, ret, acc_in, out_h, acc, out, sems):
+    )(own, table, slots, blocks, pattern, rhs)
+
+
+def assemble_kernel(where, ret, acc_in, out_h, acc, out, sems):
     del acc_in
+    fronts = where.shape[0] // 5
 
     def one_front(f, carry):
-        at = where[f]
+        at = pl.multiple_of(where[f], 8)
         for h in range(4):
-            rows = pl.ds(pl.multiple_of(blocks[h, f] * 8, 8), COLS)
-            v = ret[at, pl.ds(h, COLS, stride=4), :]
+            rows = pl.ds(pl.multiple_of(where[(h + 1) * fronts + f], 8), COLS)
+            v = ret[pl.ds(at + h, COLS, stride=4), :]
             acc[rows, :] = v if h < 2 else acc[rows, :] - v
         return carry
 
-    lax.fori_loop(0, where.shape[0], one_front, 0, unroll=8)
+    lax.fori_loop(0, fronts, one_front, 0, unroll=8)
 
     copies = []
     for j in range(COLS):
@@ -495,7 +506,7 @@
         copy.wait()
 
 
-def assemble(where, blocks, ret, acc):
+def assemble(where, ret, acc):
     vmem = pl.BlockSpec(memory_space=pltpu.VMEM)
     smem = pl.BlockSpec(memory_space=pltpu.SMEM)
     shape = (COLS * ROW_BLOCKS, BLOCK)
@@ -505,24 +516,24 @@
             jax.ShapeDtypeStruct(shape, jnp.float32),
             jax.ShapeDtypeStruct(acc.shape, jnp.float32),
         ),
-        in_specs=[smem, smem, vmem, vmem],
+        in_specs=[smem, vmem, vmem],
         out_specs=(pl.BlockSpec(memory_space=pltpu.HBM), vmem),
         scratch_shapes=[pltpu.VMEM(shape, jnp.float32), pltpu.SemaphoreType.DMA((COLS,))],
-        input_output_aliases={3: 1},
+        input_output_aliases={2: 1},
         compiler_params=pltpu.CompilerParams(vmem_limit_bytes=16 * 1024 * 1024),
         name="assemble",
-    )(where, blocks, ret, acc)[0]
+    )(where, ret, acc)[0]
 
 
 def branch(tier, own, table, slots, blocks, pattern, rhs):
-    ret, acc, where = exchange(tier, own, table, slots, pattern, rhs)
-    return assemble(where, blocks, ret.reshape(RING_SLOTS * PLANE, MSG, BLOCK), acc)
+    ret, acc, where = exchange(tier, own, table, slots, blocks, pattern, rhs)
+    return assemble(where, ret.reshape(RING_SLOTS * PLANE * MSG, BLOCK), acc)
 
 
 def on_device(rhs, pattern, front_blocks, front_slot, pivot_inverse, update_factor):
     shape = rhs.shape
     blocks = front_blocks.T
-    table, own, tier = make_tables(front_slot, blocks, pivot_inverse, update_factor)
+    table, own, tier = make_tables(front_slot, pivot_inverse, update_factor)
     out = lax.switch(
         tier[0],
         [functools.partial(branch, t) for t in TIERS],

time: 59.5 us -> 57.3 us (0.963)
  Pallas kernels: 58.7 us -> 56.6 us
    pallas_call x1, Pallas kernels: 53.6 us -> 51.7 us  [exchange(): pl.pallas_call(functools.partial(exchange_kernel, tier), out_shape=(jax.S...]
where the time goes in v5:
time: 57.3 us; the launch traced here: 57.2 us
  Pallas kernels  56.6 us (99%)
  between operations  0.66 us (1%)
    pallas_call x1, Pallas kernels, exchange(): pl.pallas_call(functools.partial(exchange_kernel, tier), out_shape=(jax.S...  51.7 us
    pallas_call x1, Pallas kernels, assemble(): pl.pallas_call(assemble_kernel, out_shape=(jax.ShapeDtypeStruct(shape, jn...  3.07 us
    pallas_call x1, Pallas kernels, make_tables(): pl.pallas_call(tables_kernel, out_shape=(jax.ShapeDtypeStruct((2 * RING_S...  1.74 us

profile of v5, /device:TPU:1, one launch (start us, length us, event | category | flops | bytes accessed | tf_op | source)
XLA Modules:
  0.0 57.2 jit_solution(3207289679576173839)
XLA Ops:
  0.0 1.7 %tables.1 = (s32[32,128]{1,0:T(8,128)S(1)}, f32[2,768,128]{2,1,0:T(8,128)S(1)}, s32[1]{0:T(128)}) custom-call(s32[128]{0:T(128)} %slots_h.1, f32[2,256,256]{2,1,0:T(8,128)} %pinv_h.1, f32[2,256,256]{2,1,0:T(8,128)} %ufac_h.1), custom_call_target="tpu_custom_call" | custom-call | tf_op jit(solution)/shard_map/tables/pallas_call | solution.py:146
  2.4 54.8 %conditional.1 = (f32[1,6,49152]{2,0,1:T(1,128)}) conditional(s32[]{:T(128)} %bitcast.12, (f32[2,768,128]{2,1,0:T(8,128)S(1)}, s32[32,128]{1,0:T(8,128)S(1)}, s32[128]{0:T(128)}, s32[4,128]{1,0:T(4,128)}, s32[384,1]{0,1:T(1,128)}, /*index=5*/f32[1,6,49152]{2,0,1:T(1,128)}) %tuple.30, (f32[2,768,128]{2,1,0:T(8,128)S(1)}, ...), branch_computations={%region_0.0_spmd, %region_1.0_spmd, %region_2.0_spmd} | conditional | bytes 8 | solution.py:537
  2.4 51.7 %exchange_12.1 = (f32[16,384,128]{2,1,0:T(8,128)S(1)}, f32[3072,128]{1,0:T(8,128)S(1)}, s32[640]{0:T(1024)S(1)}) custom-call(f32[2,768,128]{2,1,0:T(8,128)S(1)} %get-tuple-element.44.own, s32[32,128]{1,0:T(8,128)S(1)} %get-tuple-element.46.table_h, s32[128]{0:T(128)} %get-tuple-element.47.slots_h, s32[4,128]{1,0:T(4,128)} %get-tuple-element.48.blocks_h, ...), custom_call_target="tpu_custom_call" | custom-call | tf_op jit(solution)/shard_map/cond/branch_0_fun/exchange_12/pallas_call | solution.py:446
  54.2 3.1 %assemble.3 = (f32[2304,128]{1,0:T(8,128)}, f32[3072,128]{1,0:T(8,128)S(1)}) custom-call(s32[640]{0:T(1024)S(1)} %get-tuple-element.51.where, f32[6144,128]{1,0:T(8,128)S(1)} %bitcast.14, f32[3072,128]{1,0:T(8,128)S(1)} %get-tuple-element.53.acc_in), custom_call_target="tpu_custom_call", output_to_operand_aliasing={{1}: (2, {})} | custom-call | tf_op jit(solution)/shard_map/cond/branch_0_fun/assemble/pallas_call | solution.py:513

commit v6 on v5

--- a/solution.py
+++ b/solution.py
@@ -48,14 +48,17 @@
     return both[:n] + (both[n:] + dot(xh, wl))
 
 
-TIERS = (12, 14, 16)
+TIERS = (12, 13, 16)
+
+
+def pairs_from(tier):
+    return max(15 - tier, 0)
 
 
 def first_position(tier, o):
     p, a = o // 2, o % 2
-    if tier == 12:
-        return max(p - 1, 0) if p < 3 else 2 * p - 4 + a
-    return max(2 * p - (16 - tier) + a, 0) if p else a * (tier == 16)
+    start = max(2 * p - (16 - tier), p - 1, 0)
+    return start + a if p >= pairs_from(tier) else start
 
 
 def slot_in_sequence(o, z, ring):
@@ -316,7 +319,7 @@
         start_out(p)
         return carry
 
-    lax.fori_loop(0, tier // 2, out_step, 0)
+    lax.fori_loop(0, (tier + 1) // 2, out_step, 0)
 
     def init(k, carry):
         on = mask[pl.ds(pl.multiple_of(8 * k, 8), 8), :]
@@ -380,22 +383,24 @@
             forward(i, d)
             if a == 0:
 
-                @pl.when(p < tier // 2)
+                @pl.when(p < (tier + 1) // 2)
                 def _():
                     arrive(p)
 
             collect(i, d)
             solve(2 * p + a, fac.at[slot_from(i, d)])
-            if tier != 12:
-                give_back(2 * p - (16 - tier) + a)
-            elif a == 0:
-
-                @pl.when(p >= 3)
+            two = pairs_from(tier)
+            t = 2 * p - (16 - tier) + a
+            if a == 1:
+                give_back(jnp.where(p < two, p - 1, t))
+            elif two <= 2:
+                give_back(t)
+            else:
+
+                @pl.when(p >= two)
                 def _():
-                    give_back(2 * p - 4)
-
-            else:
-                give_back(jnp.where(p < 3, p - 1, 2 * p - 3))
+                    give_back(t)
+
         return carry
 
     lax.fori_loop(1, FAR, step, 0)
@@ -428,7 +433,7 @@
         wait_bytes(arr, p, PLANE - 1, out_ss.at[p])
         return carry
 
-    lax.fori_loop(0, tier // 2, drain_out, 0)
+    lax.fori_loop(0, (tier + 1) // 2, drain_out, 0)
 
     def drain_back(t, carry):
         wait_bytes(back, t, PLANE - 1, ret_ss.at[t])

time: 57.3 us -> 57.3 us (level)
  no operation moved by 1% of the time
where the time goes in v6:
time: 57.3 us; the launch traced here: 57.2 us
  Pallas kernels  56.6 us (99%)
  between operations  0.66 us (1%)
    pallas_call x1, Pallas kernels, exchange(): pl.pallas_call(functools.partial(exchange_kernel, tier), out_shape=(jax.S...  51.7 us
    pallas_call x1, Pallas kernels, assemble(): pl.pallas_call(assemble_kernel, out_shape=(jax.ShapeDtypeStruct(shape, jn...  3.07 us
    pallas_call x1, Pallas kernels, make_tables(): pl.pallas_call(tables_kernel, out_shape=(jax.ShapeDtypeStruct((2 * RING_S...  1.74 us

profile of v6, /device:TPU:1, one launch (start us, length us, event | category | flops | bytes accessed | tf_op | source)
XLA Modules:
  0.0 57.2 jit_solution(5633263995937236397)
XLA Ops:
  0.0 1.7 %tables.1 = (s32[32,128]{1,0:T(8,128)S(1)}, f32[2,768,128]{2,1,0:T(8,128)S(1)}, s32[1]{0:T(128)}) custom-call(s32[128]{0:T(128)} %slots_h.1, f32[2,256,256]{2,1,0:T(8,128)} %pinv_h.1, f32[2,256,256]{2,1,0:T(8,128)} %ufac_h.1), custom_call_target="tpu_custom_call" | custom-call | tf_op jit(solution)/shard_map/tables/pallas_call | solution.py:149
  2.4 54.8 %conditional.1 = (f32[1,6,49152]{2,0,1:T(1,128)}) conditional(s32[]{:T(128)} %bitcast.12, (f32[2,768,128]{2,1,0:T(8,128)S(1)}, s32[32,128]{1,0:T(8,128)S(1)}, s32[128]{0:T(128)}, s32[4,128]{1,0:T(4,128)}, s32[384,1]{0,1:T(1,128)}, /*index=5*/f32[1,6,49152]{2,0,1:T(1,128)}) %tuple.30, (f32[2,768,128]{2,1,0:T(8,128)S(1)}, ...), branch_computations={%region_0.0_spmd, %region_1.0_spmd, %region_2.0_spmd} | conditional | bytes 8 | solution.py:542
  2.4 51.7 %exchange_12.1 = (f32[16,384,128]{2,1,0:T(8,128)S(1)}, f32[3072,128]{1,0:T(8,128)S(1)}, s32[640]{0:T(1024)S(1)}) custom-call(f32[2,768,128]{2,1,0:T(8,128)S(1)} %get-tuple-element.44.own, s32[32,128]{1,0:T(8,128)S(1)} %get-tuple-element.46.table_h, s32[128]{0:T(128)} %get-tuple-element.47.slots_h, s32[4,128]{1,0:T(4,128)} %get-tuple-element.48.blocks_h, ...), custom_call_target="tpu_custom_call" | custom-call | tf_op jit(solution)/shard_map/cond/branch_0_fun/exchange_12/pallas_call | solution.py:451
  54.2 3.1 %assemble.3 = (f32[2304,128]{1,0:T(8,128)}, f32[3072,128]{1,0:T(8,128)S(1)}) custom-call(s32[640]{0:T(1024)S(1)} %get-tuple-element.51.where, f32[6144,128]{1,0:T(8,128)S(1)} %bitcast.14, f32[3072,128]{1,0:T(8,128)S(1)} %get-tuple-element.53.acc_in), custom_call_target="tpu_custom_call", output_to_operand_aliasing={{1}: (2, {})} | custom-call | tf_op jit(solution)/shard_map/cond/branch_0_fun/assemble/pallas_call | solution.py:518

commit v7 on v6

--- a/solution.py
+++ b/solution.py
@@ -188,11 +188,11 @@
     below = lax.rem(z + NZ - 1, NZ)
 
     barrier = pltpu.get_barrier_semaphore()
+    for zz in (above, below):
+        pl.semaphore_signal(barrier, inc=1, device_id=(chip(y, zz, x), c), device_id_type=MESH)
     for dy, dx in PEERS:
         py, px = peer(dy, dx)
         pl.semaphore_signal(barrier, inc=1, device_id=(chip(py, z, px), c), device_id_type=MESH)
-    for zz in (above, below):
-        pl.semaphore_signal(barrier, inc=1, device_id=(chip(y, zz, x), c), device_id_type=MESH)
     pl.semaphore_signal(barrier, inc=1, device_id=(r, 1 - c), device_id_type=MESH)
 
     fetches = [

time: 57.3 us -> 57.6 us (level)
  no operation moved by 1% of the time
where the time goes in v7:
time: 57.6 us; the launch traced here: 57.5 us
  Pallas kernels  56.8 us (99%)
  between operations  0.66 us (1%)
    pallas_call x1, Pallas kernels, exchange(): pl.pallas_call(functools.partial(exchange_kernel, tier), out_shape=(jax.S...  52 us
    pallas_call x1, Pallas kernels, assemble(): pl.pallas_call(assemble_kernel, out_shape=(jax.ShapeDtypeStruct(shape, jn...  3.07 us
    pallas_call x1, Pallas kernels, make_tables(): pl.pallas_call(tables_kernel, out_shape=(jax.ShapeDtypeStruct((2 * RING_S...  1.74 us

profile of v7, /device:TPU:1, one launch (start us, length us, event | category | flops | bytes accessed | tf_op | source)
XLA Modules:
  0.0 57.5 jit_solution(8843271805933730286)
XLA Ops:
  0.0 1.7 %tables.1 = (s32[32,128]{1,0:T(8,128)S(1)}, f32[2,768,128]{2,1,0:T(8,128)S(1)}, s32[1]{0:T(128)}) custom-call(s32[128]{0:T(128)} %slots_h.1, f32[2,256,256]{2,1,0:T(8,128)} %pinv_h.1, f32[2,256,256]{2,1,0:T(8,128)} %ufac_h.1), custom_call_target="tpu_custom_call" | custom-call | tf_op jit(solution)/shard_map/tables/pallas_call | solution.py:149
  2.4 55.1 %conditional.1 = (f32[1,6,49152]{2,0,1:T(1,128)}) conditional(s32[]{:T(128)} %bitcast.12, (f32[2,768,128]{2,1,0:T(8,128)S(1)}, s32[32,128]{1,0:T(8,128)S(1)}, s32[128]{0:T(128)}, s32[4,128]{1,0:T(4,128)}, s32[384,1]{0,1:T(1,128)}, /*index=5*/f32[1,6,49152]{2,0,1:T(1,128)}) %tuple.30, (f32[2,768,128]{2,1,0:T(8,128)S(1)}, ...), branch_computations={%region_0.0_spmd, %region_1.0_spmd, %region_2.0_spmd} | conditional | bytes 8 | solution.py:542
  2.4 52.0 %exchange_12.1 = (f32[16,384,128]{2,1,0:T(8,128)S(1)}, f32[3072,128]{1,0:T(8,128)S(1)}, s32[640]{0:T(1024)S(1)}) custom-call(f32[2,768,128]{2,1,0:T(8,128)S(1)} %get-tuple-element.44.own, s32[32,128]{1,0:T(8,128)S(1)} %get-tuple-element.46.table_h, s32[128]{0:T(128)} %get-tuple-element.47.slots_h, s32[4,128]{1,0:T(4,128)} %get-tuple-element.48.blocks_h, ...), custom_call_target="tpu_custom_call" | custom-call | tf_op jit(solution)/shard_map/cond/branch_0_fun/exchange_12/pallas_call | solution.py:451
  54.4 3.1 %assemble.3 = (f32[2304,128]{1,0:T(8,128)}, f32[3072,128]{1,0:T(8,128)S(1)}) custom-call(s32[640]{0:T(1024)S(1)} %get-tuple-element.51.where, f32[6144,128]{1,0:T(8,128)S(1)} %bitcast.14, f32[3072,128]{1,0:T(8,128)S(1)} %get-tuple-element.53.acc_in), custom_call_target="tpu_custom_call", output_to_operand_aliasing={{1}: (2, {})} | custom-call | tf_op jit(solution)/shard_map/cond/branch_0_fun/assemble/pallas_call | solution.py:518
